TPU v7x, 8 devices: a whole 2x2x1 slice. The times are simulated.
8 devices in a mesh: dp: 2 (over z, y), ep: 4 (over x, core).
Axes of the slice: x: 2, y: 2, z: 1, core: 2. Of those that a mesh axis runs over, the one named last changes fastest.
Arguments:
- x_norm: bfloat16 [2048, 4096], P(('dp', 'ep'))
- route_idx: int32 [2048, 4], P(('dp', 'ep'))
- w_router: bfloat16 [4096, 16], replicated
- w_gate: bfloat16 [16, 4096, 688], P('ep')
- w_up: bfloat16 [16, 4096, 688], P('ep')
- w_down: bfloat16 [16, 688, 4096], P('ep')
- grad_out: bfloat16 [2048, 4096], P(('dp', 'ep'))
Outputs:
- output 1: bfloat16 [2048, 4096], P(('dp', 'ep'))
- output 2: float32 [16, 4096, 688], P('ep')
- output 3: float32 [16, 4096, 688], P('ep')
- output 4: float32 [16, 688, 4096], P('ep')
- output 5: float32 [4096, 16], replicated
All inputs are finite; a program needn't handle non-finite values.
Results may differ from a plain program's by a relative error of at most 0.00549165.
Values are sent between devices in bfloat16 or wider.
A program may use at most 1 GiB of HBM per device.

v0:
```python
import functools

import jax
import jax.numpy as jnp
from jax import lax
from jax.experimental import pallas as pl
from jax.experimental.pallas import tpu as pltpu
from jax.sharding import PartitionSpec as P


COLD = 64
OVER = 128
VMEM_LIMIT = 62 * 1024 * 1024
F32 = jnp.float32
BF16 = jnp.bfloat16

NN = (((1,), (0,)), ((), ()))
NT = (((1,), (1,)), ((), ()))


def mm(a, b, dims):
    return lax.dot_general(a, b, dims, preferred_element_type=F32)


def tile_of(step, eidx):
    return jnp.where(step < 4, eidx[step], 4 + (step - 4) // 2)


def cost(flops, nbytes):
    return pl.CostEstimate(flops=int(flops), bytes_accessed=int(nbytes), transcendentals=0)


def dispatch_kernel(with_g, gated, slots, *refs):
    if gated:
        gates, v, refs = refs[0], refs[1:5], refs[5:]
        do_out, g_out = refs[0], (refs[1] if with_g else None)
        sel, col = refs[-2:]
    else:
        v, (x_out, sel) = refs[0:4], refs[4:]

    @pl.when(pl.program_id(0) == 0)
    def _():
        for k in range(4):
            for m in range(5):
                n = OVER if m == 4 else COLD
                lo = COLD * m
                row = lax.broadcasted_iota(jnp.int32, (n, 256), 0).astype(F32) + float(lo)
                hit = slots[k, m:m + 1, :] == row
                sel[k, lo:lo + n, :] = jnp.where(hit, 1.0, 0.0).astype(BF16)
                if gated:
                    col[k, lo:lo + n, :] = jnp.sum(jnp.where(hit, gates[k, m:m + 1, :], 0.0), axis=1, keepdims=True)

    def put(out, k, rows):
        for j in range(4):
            out[j, COLD * k:COLD * (k + 1), :] = rows[COLD * j:COLD * (j + 1)]
        out[4 + k // 2, OVER * (k % 2):OVER * (k % 2) + OVER, :] = rows[256:384]

    for k in range(4):
        rows = mm(sel[k], v[k][...], NN)
        if gated:
            put(do_out, k, (col[k] * rows).astype(BF16))
            if with_g:
                put(g_out, k, rows.astype(BF16))
        else:
            put(x_out, k, rows.astype(BF16))


def dispatch(slots, gates, vs, with_g):
    tok, dim = vs[0].shape
    dc = 512
    gated = gates is not None
    small = pl.BlockSpec((4, 8, 256), lambda c: (0, 0, 0))
    n_out = 2 if with_g else 1
    scratch = [pltpu.VMEM((4, 384, 256), BF16)]
    if gated:
        scratch.append(pltpu.VMEM((4, 384, 1), F32))
    return pl.pallas_call(
        functools.partial(dispatch_kernel, with_g, gated),
        grid=(dim // dc,),
        in_specs=[small] * (2 if gated else 1) + [pl.BlockSpec((tok, dc), lambda c: (0, c))] * 4,
        out_specs=[pl.BlockSpec((6, 256, dc), lambda c: (0, 0, c))] * n_out,
        out_shape=[jax.ShapeDtypeStruct((6, 256, dim), BF16)] * n_out,
        scratch_shapes=scratch,
        compiler_params=pltpu.CompilerParams(vmem_limit_bytes=VMEM_LIMIT),
        cost_estimate=cost(2 * 1536 * 256 * dim, 2 * n_out * 1536 * dim * 2),
        name="dispatch",
    )(*([slots, gates] if gated else [slots]), *vs)


def tile_kernel_call(kernel, eidx, act, rows, weights, late, outs, n_mm):
    ff, dim = weights[0].shape[1:]
    dc = 2048
    n_c = dim // dc

    def last(c, i, e):
        return jnp.where(c == n_c - 1, tile_of(i, e), tile_of(0, e))

    row_blk = pl.BlockSpec((1, 256, dc), lambda c, i, e, t: (tile_of(i, e), 0, c))
    w_blk = pl.BlockSpec((1, ff, dc), lambda c, i, e, t: (e[i], 0, c))
    late_blk = pl.BlockSpec((1, ff, 256), lambda c, i, e, t: (last(c, i, e), 0, 0))
    return pl.pallas_call(
        functools.partial(kernel, n_c),
        grid_spec=pltpu.PrefetchScalarGridSpec(
            num_scalar_prefetch=2, grid=(n_c, 8),
            in_specs=[row_blk] * len(rows) + [w_blk] * len(weights) + [late_blk] * len(late),
            out_specs=[pl.BlockSpec((1,) + o.shape[1:], lambda c, i, e, t: (last(c, i, e), 0, 0)) for o in outs],
            scratch_shapes=[pltpu.VMEM((8, ff, 256), F32)] * n_mm),
        out_shape=outs,
        compiler_params=pltpu.CompilerParams(vmem_limit_bytes=VMEM_LIMIT),
        cost_estimate=cost(n_mm * 2 * 1536 * dim * ff, 80e6),
    )(eidx, act, *rows, *weights, *late)


def accumulate(act, acc, terms, n_c, finish):
    c, step = pl.program_id(0), pl.program_id(1)

    @pl.when(act[step] == 1)
    def _():
        for ref, val in zip(acc, terms()):
            ref[step] = jnp.where(c == 0, 0.0, ref[step]) + val

    @pl.when((act[step] == 1) & (c == n_c - 1))
    def _():
        @pl.when((step != 5) & (step != 7))
        def _():
            finish(step, 0)

        finish(step, 128)


def forward_kernel(n_c, eidx, act, x, w1, w3, s_out, zu_out, sp_out, a_out, z1, z3):
    def terms():
        yield mm(w1[0], x[0], NT)
        yield mm(w3[0], x[0], NT)

    def finish(step, lo):
        n = 128
        z_gate, z_up = z1[step, :, lo:lo + n], z3[step, :, lo:lo + n]
        sig = jax.nn.sigmoid(z_gate)
        silu = z_gate * sig
        s_out[0, :, lo:lo + n] = silu
        zu_out[0, :, lo:lo + n] = z_up
        sp_out[0, :, lo:lo + n] = sig * (1.0 + z_gate * (1.0 - sig))
        a_out[0, :, lo:lo + n] = (silu * z_up).astype(BF16)

    accumulate(act, (z1, z3), terms, n_c, finish)


def hidden_grad_kernel(with_g, n_c, eidx, act, *refs):
    if with_g:
        do, g, w2, s_in, zu_in, sp_in, a_in, d1_out, d3_out, q_out, d1r_out, d3r_out, da, hg = refs
    else:
        do, w2, s_in, zu_in, sp_in, d1_out, d3_out, da = refs

    def terms():
        yield mm(w2[0], do[0], NT)
        if with_g:
            yield mm(w2[0], g[0], NT)

    def finish(step, lo):
        n = 128
        d_act = da[step, :, lo:lo + n]
        d1 = (d_act * zu_in[0, :, lo:lo + n] * sp_in[0, :, lo:lo + n]).astype(BF16)
        d3 = (d_act * s_in[0, :, lo:lo + n]).astype(BF16)
        d1_out[0, :, lo:lo + n] = d1
        d3_out[0, :, lo:lo + n] = d3
        if with_g:
            a = a_in[0, :, lo:lo + n].astype(F32)
            q = jnp.sum(a * hg[step, :, lo:lo + n], axis=0, keepdims=True)
            q_out[0, :, lo:lo + n] = jnp.broadcast_to(q, (8, n))
            d1r_out[0, lo:lo + n, :] = d1.astype(F32).T.astype(BF16)
            d3r_out[0, lo:lo + n, :] = d3.astype(F32).T.astype(BF16)

    accumulate(act, (da, hg) if with_g else (da,), terms, n_c, finish)


def forward(eidx, act, x, w1t, w3t):
    ff = w1t.shape[1]
    outs = [jax.ShapeDtypeStruct((6, ff, 256), F32)] * 3 + [jax.ShapeDtypeStruct((6, ff, 256), BF16)]
    return tile_kernel_call(forward_kernel, eidx, act, [x], [w1t, w3t], [], outs, 2)


def hidden_grad(eidx, act, rows, w2, late):
    ff = w2.shape[1]
    with_g = len(rows) == 2
    outs = [jax.ShapeDtypeStruct((6, ff, 256), BF16)] * 2
    if with_g:
        outs += [jax.ShapeDtypeStruct((6, 8, 256), F32)] + [jax.ShapeDtypeStruct((6, 256, ff), BF16)] * 2
    kernel = functools.partial(hidden_grad_kernel, with_g)
    return tile_kernel_call(kernel, eidx, act, rows, [w2], late, outs, len(rows))


def back_kernel(eidx, act, d1, d3, w1, w3, s0, s1, s2, s3, o0, o1, o2, o3, r_sc):
    step = pl.program_id(1)
    slots, outs = (s0, s1, s2, s3), (o0, o1, o2, o3)

    def rows(cols):
        r = (mm(d1[0], w1[0, :, cols], NN) + mm(d3[0], w3[0, :, cols], NN)).astype(BF16)

        @pl.when(step < 4)
        def _():
            lo = pl.multiple_of(eidx[step] * COLD, COLD)
            for k in range(4):
                r_sc[k, pl.ds(lo, COLD), cols] = r[COLD * k:COLD * (k + 1)]

        for q in range(2):
            @pl.when(step == 4 + 2 * q)
            def _():
                r_sc[2 * q, 256:384, cols] = r[0:128]

            @pl.when((step == 4 + 2 * q) | (step == 5 + 2 * q))
            def _():
                r_sc[2 * q + 1, 256:384, cols] = r[128:256]

    @pl.when(act[step] == 1)
    def _():
        def body(h, _):
            rows(pl.ds(pl.multiple_of(h * 1024, 1024), 1024))
            return 0

        lax.fori_loop(0, w1.shape[2] // 1024, body, 0)

    @pl.when(step == 7)
    def _():
        lane = lax.broadcasted_iota(jnp.int32, (256, 384), 1).astype(F32)
        for k in range(4):
            hit = lane == slots[k][:, 0:1]
            for m in range(1, 5):
                hit = hit | (lane == slots[k][:, m:m + 1])
            sel = jnp.where(hit, 1.0, 0.0).astype(BF16)
            outs[k][...] = mm(sel, r_sc[k], NN)


def back(eidx, act, d1, d3, w1t, w3t, slots):
    ff, dim = w1t.shape[1:]
    dc = 2048

    d_blk = pl.BlockSpec((1, 256, ff), lambda c, i, e, t: (tile_of(i, e), 0, 0))
    w_blk = pl.BlockSpec((1, ff, dc), lambda c, i, e, t: (e[i], 0, c))
    s_blk = pl.BlockSpec((256, 8), lambda c, i, e, t: (0, 0))
    o_blk = pl.BlockSpec((256, dc), lambda c, i, e, t: (0, c))
    return pl.pallas_call(
        back_kernel,
        grid_spec=pltpu.PrefetchScalarGridSpec(
            num_scalar_prefetch=2, grid=(dim // dc, 8),
            in_specs=[d_blk, d_blk, w_blk, w_blk] + [s_blk] * 4, out_specs=[o_blk] * 4,
            scratch_shapes=[pltpu.VMEM((4, 384, dc), BF16)]),
        out_shape=[jax.ShapeDtypeStruct((256, dim), F32)] * 4,
        compiler_params=pltpu.CompilerParams(vmem_limit_bytes=VMEM_LIMIT),
        cost_estimate=cost(2 * 2 * 1536 * dim * ff, 70e6),
        name="back",
    )(eidx, act, d1, d3, w1t, w3t, *slots)


def wgrad_kernel(info, xa, xb, ga, gb, xoa, xob, goa, gob,
                 aa, d1a, d3a, ab, d1b, d3b, aoa, d1oa, d3oa, aob, d1ob, d3ob, w1o, w3o, w2o):
    j = pl.program_id(0)
    all_hot = info[1] == j
    for m in range(2, 9):
        all_hot = all_hot & (info[m] == j)

    def run(first, second, cols):
        def part(n, q):
            x, g, a, d1, d3 = n
            return x[q, :, cols], g[q, :, cols], a[q], d1[q], d3[q]

        def products(parts):
            w1o[0, :, cols] = sum(mm(p[3], p[0], NN) for p in parts)
            w3o[0, :, cols] = sum(mm(p[4], p[0], NN) for p in parts)
            w2o[0, :, cols] = sum(mm(p[2], p[1], NN) for p in parts)

        main = [part(first[0], 0), part(second[0], 0)]

        @pl.when(all_hot)
        def _():
            products(main + [part(n[1], q) for n in (first, second) for q in range(2)])

        @pl.when(jnp.logical_not(all_hot))
        def _():
            products(main)
            for _, over, off in (first, second):

                def body(q, _):
                    h0, h1 = info[off + 2 * q], info[off + 2 * q + 1]

                    @pl.when((h0 == j) | (h1 == j))
                    def _():
                        x, g, a, d1, d3 = part(over, q)
                        row = lax.broadcasted_iota(jnp.int32, a.shape, 1)
                        mine = jnp.where(row < 128, h0, h1) == j

                        def keep(v):
                            return jnp.where(mine, v.astype(F32), 0.0).astype(BF16)

                        w1o[0, :, cols] += mm(keep(d1), x, NN)
                        w3o[0, :, cols] += mm(keep(d3), x, NN)
                        w2o[0, :, cols] += mm(keep(a), g, NN)

                    return 0

                lax.fori_loop(0, 2, body, 0)

    na = ((xa, ga, aa, d1a, d3a), (xoa, goa, aoa, d1oa, d3oa), 1)
    nb = ((xb, gb, ab, d1b, d3b), (xob, gob, aob, d1ob, d3ob), 5)

    def columns(h, _):
        cols = pl.ds(pl.multiple_of(h * 512, 512), 512)

        @pl.when(info[0] == 0)
        def _():
            run(na, nb, cols)

        @pl.when(info[0] == 1)
        def _():
            run(nb, na, cols)

        return 0

    lax.fori_loop(0, w1o.shape[2] // 512, columns, 0)


def wgrad(info, xa, ga, hid_a, xb, gb, hid_b, dim, ff):
    dc = 1024

    def over(off):
        def index(j, c, s):
            used = (s[off] == j) | (s[off + 1] == j) | (s[off + 2] == j) | (s[off + 3] == j)
            return 2, 0, jnp.where(used, c, 0)

        return pl.BlockSpec((2, 256, dc), index)

    main_blk = pl.BlockSpec((1, 256, dc), lambda j, c, s: (j, 0, c))
    hid_blk = pl.BlockSpec((1, ff, 256), lambda j, c, s: (j, 0, 0))
    hid_over = pl.BlockSpec((2, ff, 256), lambda j, c, s: (2, 0, 0))
    return pl.pallas_call(
        wgrad_kernel,
        grid_spec=pltpu.PrefetchScalarGridSpec(
            num_scalar_prefetch=1, grid=(4, dim // dc),
            in_specs=[main_blk] * 4 + [over(1), over(5)] * 2 + [hid_blk] * 6 + [hid_over] * 6,
            out_specs=[pl.BlockSpec((1, ff, dc), lambda j, c, s: (j, 0, c))] * 3),
        out_shape=[jax.ShapeDtypeStruct((4, ff, dim), F32)] * 3,
        compiler_params=pltpu.CompilerParams(vmem_limit_bytes=VMEM_LIMIT),
        cost_estimate=cost(3 * 2 * 3072 * dim * ff, 200e6),
        name="wgrad",
    )(info, xa, xb, ga, gb, xa, xb, ga, gb, *hid_a, *hid_b, *hid_a, *hid_b)


def solution(mesh):
    tok_spec = P(("dp", "ep"), None)
    exp_spec = P("ep", None, None)
    axes = ("dp", "ep")

    def shift(arr, dp_bit, ep_bits):
        pairs = [(s, (((s // 4) ^ dp_bit) * 4) + ((s % 4) ^ ep_bits)) for s in range(8)]
        return lax.ppermute(arr, axes, pairs)

    def device_step(x_loc, route_idx, w_router, w_gate, w_up, w_down, dy_loc):
        tok, dim = x_loc.shape
        ff = w_gate.shape[2]
        ep = lax.axis_index("ep")
        dp = lax.axis_index("dp")
        e0 = ep * 4
        w1t, w3t, w2 = jnp.swapaxes(w_gate, 1, 2), jnp.swapaxes(w_up, 1, 2), w_down

        order = jnp.arange(tok, dtype=jnp.int32)
        before = (order[:, None] < order[None, :]).astype(BF16)
        local = jnp.arange(4, dtype=jnp.int32)

        def tables(idx):
            picked = jnp.any(idx[:, None] == (e0 + local)[None, :, None, None], axis=2)
            ranks = jnp.dot(picked.reshape(16, tok).astype(BF16), before, preferred_element_type=F32)
            ranks = jnp.where(picked, ranks.reshape(4, 4, tok), -1.0)
            main = jnp.where((ranks >= 0) & (ranks < COLD), ranks + COLD * local.astype(F32)[None, :, None], -1.0)
            over = jnp.max(jnp.where(ranks >= COLD, ranks - COLD + 4 * COLD, -1.0), axis=1, keepdims=True)
            slots = jnp.concatenate([main, over, jnp.full((4, 3, tok), -1.0, F32)], axis=1)
            large = jnp.max(ranks, axis=2) >= COLD
            hot = jnp.min(jnp.where(large, local[None, :], 3), axis=1)
            first = jnp.arange(3, dtype=jnp.int32)
            first = first + (first >= hot[0])
            eidx = jnp.concatenate([first, hot[:1], hot])
            one = jnp.ones((), jnp.int32)
            act = jnp.stack([one, one, one, one, one, (hot[0] != hot[1]).astype(jnp.int32),
                             one, (hot[2] != hot[3]).astype(jnp.int32)])
            return ranks, slots, hot, eidx, act

        def gate_table(gates, ranks):
            mine = jnp.stack([lax.dynamic_slice_in_dim(v, e0, 4, axis=0) for v in gates])
            over = jnp.sum(jnp.where(ranks >= COLD, mine, 0.0), axis=1, keepdims=True)
            return jnp.concatenate([mine, over, jnp.zeros((4, 3, tok), F32)], axis=1)

        idx_t = route_idx.T
        idx_a = jnp.stack([idx_t] + [shift(idx_t, 0, k) for k in (1, 2, 3)])
        x_across = shift(x_loc, 0, 2)
        x_sib = shift(x_loc, 0, 1)
        x_y = shift(x_loc, 1, 0)
        g_across = shift(dy_loc, 0, 2)
        g_sib = shift(dy_loc, 0, 1)
        g_y = shift(dy_loc, 1, 0)
        idx_b = jnp.stack([shift(idx_t, 1, k) for k in range(4)])

        logits = jnp.dot(x_loc, w_router, preferred_element_type=F32)
        hit = route_idx[:, :, None] == jnp.arange(16, dtype=jnp.int32)
        chosen = jnp.sum(jnp.where(hit, logits[:, None, :], 0.0), axis=2)
        probs = jax.nn.softmax(chosen, axis=-1)
        gate_t = jnp.sum(jnp.where(hit, probs[:, :, None], 0.0), axis=1).T
        gates_a = [gate_t] + [shift(gate_t, 0, k) for k in (1, 2, 3)]
        gates_b = [shift(gate_t, 1, k) for k in range(4)]

        ranks_a, slots_a, hot_a, eidx_a, act_a = tables(idx_a)
        x_across_sib = shift(x_across, 0, 1)
        x_ya = shift(x_across, 1, 0)
        x_ys = shift(x_y, 0, 1)
        xa, = dispatch(slots_a, None, (x_loc, x_sib, x_across, x_across_sib), False)
        s_a, zu_a, sp_a, a_a = forward(eidx_a, act_a, xa, w1t, w3t)
        a_a, g_across, g_y, gates_a, gates_b, idx_b = lax.optimization_barrier((a_a, g_across, g_y, gates_a, gates_b, idx_b))
        ranks_b, slots_b, hot_b, eidx_b, act_b = tables(idx_b)
        g_across_sib = shift(g_across, 0, 1)
        g_ya = shift(g_across, 1, 0)
        g_ys = shift(g_y, 0, 1)
        da, ga = dispatch(slots_a, gate_table(gates_a, ranks_a), (dy_loc, g_sib, g_across, g_across_sib), True)
        d1_a, d3_a, q_a, d1r_a, d3r_a = hidden_grad(eidx_a, act_a, (da, ga), w2, (s_a, zu_a, sp_a, a_a))
        slots_t = jnp.swapaxes(slots_a, 1, 2)
        part = back(eidx_a, act_a, d1r_a, d3r_a, w1t, w3t, [slots_t[k] for k in range(4)])

        q_rows = q_a[:, 0, :]
        q_main = q_rows[:4].reshape(4, 4, COLD).transpose(1, 0, 2)
        q_over = q_rows[4:].reshape(4, OVER)
        r64 = jnp.arange(COLD, dtype=F32)
        r128 = jnp.arange(OVER, dtype=F32) + COLD
        q_tok = jnp.sum(jnp.where(ranks_a[..., None] == r64, q_main[:, :, None, :], 0.0), axis=3)
        q_tok = q_tok + jnp.sum(jnp.where(ranks_a[..., None] == r128, q_over[:, None, None, :], 0.0), axis=3)
        q_recv = [shift(q_tok[k], 0, k) for k in (1, 2, 3)]

        part_own, x_ya, q_recv = lax.optimization_barrier((part[0], x_ya, q_recv))
        x_yas = shift(x_ya, 0, 1)

        to_sib = shift(part[1], 0, 1)
        pair = part[2] + shift(part[3], 0, 1)

        q_back = jnp.stack([q_tok[0]] + q_recv)
        q16 = q_back[ep ^ local].reshape(16, tok)
        d_sel = gate_t * (q16 - jnp.sum(gate_t * q16, axis=0, keepdims=True))
        d_logits = d_sel.astype(BF16)
        gr = jnp.dot(d_logits, x_loc, preferred_element_type=F32)

        x_yas, pair, gr = lax.optimization_barrier((x_yas, pair, gr))
        from_across = shift(pair, 0, 2)
        gr_recv = shift(gr, 0, 1)
        xb, = dispatch(slots_b, None, (x_y, x_ys, x_ya, x_yas), False)
        s_b, zu_b, sp_b, a_b = forward(eidx_b, act_b, xb, w1t, w3t)
        a_b, s_b, g_ya, gr_recv = lax.optimization_barrier((a_b, s_b, g_ya, gr_recv))
        g_yas = shift(g_ya, 0, 1)
        gr = gr + gr_recv
        gr_recv = shift(gr, 1, 0)
        db, = dispatch(slots_b, gate_table(gates_b, ranks_b), (g_y, g_ys, g_ya, g_yas), False)
        d1_b, d3_b = hidden_grad(eidx_b, act_b, (db,), w2, (s_b, zu_b, sp_b))
        d1_b, gr_recv = lax.optimization_barrier((d1_b, gr_recv))
        gr = gr + gr_recv
        gr_recv = shift(gr, 0, 2)
        info = jnp.concatenate([dp[None].astype(jnp.int32), hot_a, hot_b])
        g1t, g3t, grad_down = wgrad(info, xa, da, (a_a, d1_a, d3_a), xb, db, (a_b, d1_b, d3_b), dim, ff)
        g1t, gr_recv, from_across, d_logits = lax.optimization_barrier((g1t, gr_recv, from_across, d_logits))
        grad_router = (gr + gr_recv).T
        du = lax.dot_general(d_logits, w_router, (((0,), (1,)), ((), ())), preferred_element_type=F32)
        grad_x = (part_own + to_sib + from_across + du).astype(BF16)
        return grad_x, jnp.swapaxes(g1t, 1, 2), jnp.swapaxes(g3t, 1, 2), grad_down, grad_router

    return jax.shard_map(device_step, mesh=mesh, in_specs=(tok_spec, tok_spec, P(), exp_spec, exp_spec, exp_spec, tok_spec), out_specs=(tok_spec, exp_spec, exp_spec, exp_spec, P()), check_vma=False)
```

profile of v0, /device:TPU:0, one launch (start us, length us, event | category | flops | bytes accessed | tf_op | source)
XLA Modules:
  0.0 526.2 jit_solution(2255491422614741878)
XLA Ops:
  0.7 3.3 collective-permute-start.4
  4.0 1.2 collective-permute-start.1
  5.9 2.2 fusion.16
  8.1 0.7 select_reduce_fusion.3
  8.8 41.1 %collective-permute-done.4.refs_2_ = bf16[256,4096]{1,0:T(8,128)(2,1)S(1)} collective-permute-done((bf16[256,4096]{1,0:T(8,128)(2,1)}, bf16[256,4096]{1,0:T(8,128)(2,1)S(1)}, u32[]{:S(2)}, u32[]{:S(2)}) %collective-permute-start.4) | collective-permute-done | bytes 2097184 | tf_op jit(solution)/shard_map/ppermute | solution.py:355
  49.9 1.3 copy-done.2
  52.1 2.7 collective-permute-start.17
  55.1 1.5 collective-permute-start.15
  56.7 0.7 pad_add_fusion
  59.1 1.1 collective-permute-start.7
  60.2 1.5 collective-permute-start.6
  61.9 0.9 collective-permute-start.14
  64.1 1.3 pad_add_fusion.2.eidx
  68.6 40.8 %collective-permute-done.14 = f32[16,256]{1,0:T(8,128)S(1)} collective-permute-done((f32[16,256]{1,0:T(8,128)S(1)}, f32[16,256]{1,0:T(8,128)S(1)}, u32[]{:S(2)}, u32[]{:S(2)}) %collective-permute-start.14) | collective-permute-done | bytes 16416 | tf_op jit(solution)/shard_map/ppermute | solution.py:355
  110.7 1.4 collective-permute-start.11
  112.1 11.7 %dispatch.4.x.xa.xoa = bf16[6,256,4096]{2,1,0:T(8,128)(2,1)} custom-call(f32[4,8,256]{2,1,0:T(8,128)} %get-tuple-element.123.slots, bf16[256,4096]{1,0:T(8,128)(2,1)} %refs_0_.1, bf16[256,4096]{1,0:T(8,128)(2,1)} %collective-permute-done.3.refs_1_, bf16[256,4096]{1,0:T(8,128)(2,1)} %copy-done.2, bf16[256,4096]{1,0:T(8,128)(2,1)} %collective-permute-done.5.refs_3_), custom_call_target="tpu_custom_call" | custom-call | flops 3221225472 | bytes 25165824 | tf_op jit(solution)/shard_map/dispatch/pallas_call | solution.py:77
  124.4 1.0 collective-permute-start.9
  125.6 38.8 %shard_map.110 = (f32[6,688,256]{2,1,0:T(8,128)}, f32[6,688,256]{2,1,0:T(8,128)}, f32[6,688,256]{2,1,0:T(8,128)}, bf16[6,688,256]{2,1,0:T(8,128)(2,1)}) custom-call(s32[8]{0:T(128)} %pad_add_fusion.2.eidx, s32[8]{0:T(128)} %stack.99.act, bf16[6,256,4096]{2,1,0:T(8,128)(2,1)} %dispatch.4.x.xa.xoa, bf16[4,688,4096]{2,1,0:T(8,128)(2,1)} %bitcast.109, ...), custom_call_target="tpu_custom_call" | custom-call | flops 17314086912 | bytes 80000000 | tf_op jit(solution)/shard_map/pallas_call | solution.py:101
  165.1 0.8 copy.22.s3
  165.9 0.8 copy.21.s2
  166.7 0.8 copy.20.s1
  167.5 0.8 copy.19.s0
  170.1 1.8 collective-permute-done.20.refs_4_
  172.0 13.7 %dispatch.5 = (bf16[6,256,4096]{2,1,0:T(8,128)(2,1)}, bf16[6,256,4096]{2,1,0:T(8,128)(2,1)}) custom-call(f32[4,8,256]{2,1,0:T(8,128)} %get-tuple-element.123.slots, f32[4,8,256]{2,1,0:T(8,128)} %get-tuple-element.135.refs_0_, bf16[256,4096]{1,0:T(8,128)(2,1)} %refs_1_.2, bf16[256,4096]{1,0:T(8,128)(2,1)} %collective-permute-done.19.refs_2_, ...), custom_call_target="tpu_custom_call" | custom-call | flops 3221225472 | bytes 50331648 | tf_op jit(solution)/shard_map/dispatch/pallas_call | solution.py:77
  185.7 39.7 %shard_map.111 = (bf16[6,688,256]{2,1,0:T(8,128)(2,1)}, bf16[6,688,256]{2,1,0:T(8,128)(2,1)}, f32[6,8,256]{2,1,0:T(8,128)}, bf16[6,256,688]{2,1,0:T(8,128)(2,1)}, bf16[6,256,688]{2,1,0:T(8,128)(2,1)}) custom-call(s32[8]{0:T(128)} %pad_add_fusion.2.eidx, s32[8]{0:T(128)} %stack.99.act, bf16[6,256,4096]{2,1,0:T(8,128)(2,1)} %get-tuple-element.65.refs_0_.ga.goa, ...), custom_call_target="tpu_custom_call" | custom-call | flops 17314086912 | bytes 80000000 | tf_op jit(solution)/shard_map/pallas_call | solution.py:101
  225.4 46.6 %back.1 = (f32[256,4096]{1,0:T(8,128)}, f32[256,4096]{1,0:T(8,128)}, f32[256,4096]{1,0:T(8,128)}, f32[256,4096]{1,0:T(8,128)}) custom-call(s32[8]{0:T(128)} %pad_add_fusion.2.eidx, s32[8]{0:T(128)} %stack.99.act, bf16[6,256,688]{2,1,0:T(8,128)(2,1)} %get-tuple-element.71.d1, bf16[6,256,688]{2,1,0:T(8,128)(2,1)} %get-tuple-element.72.d3, ...), custom_call_target="tpu_custom_call" | custom-call | flops 17314086912 | bytes 70000000 | tf_op jit(solution)/shard_map/back/pallas_call | solution.py:242
  272.2 0.8 collective-permute-start.26
  273.8 0.8 slice_reduce_fusion
  274.9 1.3 select_reduce_fusion
  276.2 1.5 collective-permute-start.24
  278.4 0.9 collective-permute-done.24
  279.3 2.0 collective-permute-done.23
  281.3 39.0 %collective-permute-done.26.refs_0_ = bf16[256,4096]{1,0:T(8,128)(2,1)S(1)} collective-permute-done((bf16[256,4096]{1,0:T(8,128)(2,1)}, bf16[256,4096]{1,0:T(8,128)(2,1)S(1)}, u32[]{:S(2)}, u32[]{:S(2)}) %collective-permute-start.26) | collective-permute-done | bytes 2097184 | tf_op jit(solution)/shard_map/ppermute | solution.py:355
  325.8 1.3 pad_add_fusion.4.eidx
  328.4 2.0 fusion.17
  330.3 6.1 %add.116 = f32[256,4096]{1,0:T(8,128)} add(f32[256,4096]{1,0:T(8,128)} %get-tuple-element.79, f32[256,4096]{1,0:T(8,128)} %collective-permute-done.29) | non-fusion elementwise | flops 1048576 | bytes 12582912 | tf_op jit(solution)/shard_map/add | solution.py:438
  336.7 12.0 %dispatch.6.x.xb.xob = bf16[6,256,4096]{2,1,0:T(8,128)(2,1)} custom-call(f32[4,8,256]{2,1,0:T(8,128)} %maximum_maximum_fusion.2.slots, bf16[256,4096]{1,0:T(8,128)(2,1)} %copy-done.3, bf16[256,4096]{1,0:T(8,128)(2,1)} %collective-permute-done.27.refs_1_, bf16[256,4096]{1,0:T(8,128)(2,1)} %collective-permute-done.21.refs_2_, ...), custom_call_target="tpu_custom_call" | custom-call | flops 3221225472 | bytes 25165824 | tf_op jit(solution)/shard_map/dispatch/pallas_call | solution.py:77
  348.7 38.8 %shard_map.112 = (f32[6,688,256]{2,1,0:T(8,128)}, f32[6,688,256]{2,1,0:T(8,128)}, f32[6,688,256]{2,1,0:T(8,128)}, bf16[6,688,256]{2,1,0:T(8,128)(2,1)}) custom-call(s32[8]{0:T(128)} %pad_add_fusion.4.eidx, s32[8]{0:T(128)} %stack.121.act, bf16[6,256,4096]{2,1,0:T(8,128)(2,1)} %dispatch.6.x.xb.xob, bf16[4,688,4096]{2,1,0:T(8,128)(2,1)} %bitcast.111, ...), custom_call_target="tpu_custom_call" | custom-call | flops 17314086912 | bytes 80000000 | tf_op jit(solution)/shard_map/pallas_call | solution.py:101
  388.6 2.0 collective-permute-start.36
  391.1 0.9 collective-permute-done.33.refs_4_
  392.1 11.9 %dispatch.7.refs_0_.gb.gob = bf16[6,256,4096]{2,1,0:T(8,128)(2,1)} custom-call(f32[4,8,256]{2,1,0:T(8,128)} %maximum_maximum_fusion.2.slots, f32[4,8,256]{2,1,0:T(8,128)} %get-tuple-element.134.refs_0_, bf16[256,4096]{1,0:T(8,128)(2,1)} %collective-permute-done.7.refs_1_, bf16[256,4096]{1,0:T(8,128)(2,1)} %collective-permute-done.30.refs_2_, ...), custom_call_target="tpu_custom_call" | custom-call | flops 3221225472 | bytes 25165824 | tf_op jit(solution)/shard_map/dispatch/pallas_call | solution.py:77
  403.9 27.8 %shard_map.113 = (bf16[6,688,256]{2,1,0:T(8,128)(2,1)}, bf16[6,688,256]{2,1,0:T(8,128)(2,1)}) custom-call(s32[8]{0:T(128)} %pad_add_fusion.4.eidx, s32[8]{0:T(128)} %stack.121.act, bf16[6,256,4096]{2,1,0:T(8,128)(2,1)} %dispatch.7.refs_0_.gb.gob, bf16[4,688,4096]{2,1,0:T(8,128)(2,1)} %refs_1_.3, f32[6,688,256]{2,1,0:T(8,128)} %get-tuple-element.97.refs_2_, ...), custom_call_target="tpu_custom_call" | custom-call | flops 8657043456 | bytes 80000000 | tf_op jit(solution)/shard_map/pallas_call | solution.py:101
  431.7 2.0 collective-permute-start.35
  433.7 84.1 %wgrad.1 = (f32[4,688,4096]{2,1,0:T(8,128)}, f32[4,688,4096]{2,1,0:T(8,128)}, f32[4,688,4096]{2,1,0:T(8,128)}) custom-call(s32[9]{0:T(128)} %pad_add_fusion.3.info, bf16[6,256,4096]{2,1,0:T(8,128)(2,1)} %dispatch.4.x.xa.xoa, bf16[6,256,4096]{2,1,0:T(8,128)(2,1)} %dispatch.6.x.xb.xob, bf16[6,256,4096]{2,1,0:T(8,128)(2,1)} %get-tuple-element.65.refs_0_.ga.goa, ...), custom_call_target="tpu_custom_call" | custom-call | flops 51942260736 | bytes 200000000 | tf_op jit(solution)/shard_map/wgrad/pallas_call | solution.py:335
  517.9 0.7 fusion.18
  518.6 0.7 add_bitcast_fusion
  519.3 0.8 copy-done.1
  520.2 6.1 %add_convert_fusion = bf16[256,4096]{1,0:T(8,128)(2,1)} fusion(f32[256,4096]{1,0:T(8,128)S(1)} %fusion.18, f32[256,4096]{1,0:T(8,128)} %collective-permute-done.36, f32[256,4096]{1,0:T(8,128)S(1)} %copy-done.1, f32[256,4096]{1,0:T(8,128)} %collective-permute-done.25), kind=kLoop, calls=%fused_computation.1 | loop fusion | flops 4194304 | bytes 18874368 | tf_op jit(solution)/shard_map/convert_element_type | solution.py:465
  (118 shorter events, 18.5 us)
Async XLA Ops:
  0.6 5.2 copy-start
  0.6 57.3 %copy-start.4 = (s32[256,4]{0,1:T(4,128)S(1)}, s32[256,4]{0,1:T(4,128)}, u32[]{:S(2)}) copy-start(s32[256,4]{0,1:T(4,128)} %param.8) | copy-start | bytes 12292
  0.7 49.3 %collective-permute-start.4 = (bf16[256,4096]{1,0:T(8,128)(2,1)}, bf16[256,4096]{1,0:T(8,128)(2,1)S(1)}, u32[]{:S(2)}, u32[]{:S(2)}) collective-permute-start(bf16[256,4096]{1,0:T(8,128)(2,1)} %refs_0_.1), channel_id=1, source_target_pairs={{0,2},{1,3},{2,0},{3,1},{4,6},{5,7},{6,4},{7,5}} | collective-permute-start | bytes 6291464 | tf_op jit(solution)/shard_map/ppermute | solution.py:355
  4.0 48.1 %collective-permute-start.2 = (s32[4,256]{1,0:T(4,128)}, s32[4,256]{1,0:T(4,128)S(1)}, u32[]{:S(2)}, u32[]{:S(2)}) collective-permute-start(s32[4,256]{1,0:T(4,128)} %bitcast.89), channel_id=1, source_target_pairs={{0,3},{1,2},{2,1},{3,0},{4,7},{5,6},{6,5},{7,4}} | collective-permute-start | bytes 12296 | tf_op jit(solution)/shard_map/ppermute | solution.py:355
  4.0 50.8 %collective-permute-start.1 = (s32[4,256]{1,0:T(4,128)}, s32[4,256]{1,0:T(4,128)S(1)}, u32[]{:S(2)}, u32[]{:S(2)}) collective-permute-start(s32[4,256]{1,0:T(4,128)} %bitcast.90), channel_id=1, source_target_pairs={{0,2},{1,3},{2,0},{3,1},{4,6},{5,7},{6,4},{7,5}} | collective-permute-start | bytes 12296 | tf_op jit(solution)/shard_map/ppermute | solution.py:355
  5.2 50.0 %collective-permute-start = (s32[4,256]{1,0:T(4,128)}, s32[4,256]{1,0:T(4,128)S(1)}, u32[]{:S(2)}, u32[]{:S(2)}) collective-permute-start(s32[4,256]{1,0:T(4,128)} %bitcast.91), channel_id=1, source_target_pairs={{0,1},{1,0},{2,3},{3,2},{4,5},{5,4},{6,7},{7,6}} | collective-permute-start | bytes 12296 | tf_op jit(solution)/shard_map/ppermute | solution.py:355
  5.8 104.3 %collective-permute-start.3 = (bf16[256,4096]{1,0:T(8,128)(2,1)}, bf16[256,4096]{1,0:T(8,128)(2,1)}, u32[]{:S(2)}, u32[]{:S(2)}) collective-permute-start(bf16[256,4096]{1,0:T(8,128)(2,1)} %refs_0_.1), channel_id=1, source_target_pairs={{0,1},{1,0},{2,3},{3,2},{4,5},{5,4},{6,7},{7,6}} | collective-permute-start | bytes 6291464 | tf_op jit(solution)/shard_map/ppermute | solution.py:355
  49.9 1.3 copy-start.2
  51.2 59.5 %collective-permute-start.5 = (bf16[256,4096]{1,0:T(8,128)(2,1)S(1)}, bf16[256,4096]{1,0:T(8,128)(2,1)}, u32[]{:S(2)}, u32[]{:S(2)}) collective-permute-start(bf16[256,4096]{1,0:T(8,128)(2,1)S(1)} %collective-permute-done.4.refs_2_), channel_id=1, source_target_pairs={{0,1},{1,0},{2,3},{3,2},{4,5},{5,4},{6,7},{7,6}} | collective-permute-start | bytes 6291464 | tf_op jit(solution)/shard_map/ppermute | solution.py:355
  52.1 5.8 %collective-permute-start.17 = (s32[4,256]{1,0:T(4,128)}, s32[4,256]{1,0:T(4,128)S(1)}, u32[]{:S(2)}, u32[]{:S(2)}) collective-permute-start(s32[4,256]{1,0:T(4,128)} %bitcast.92), channel_id=1, source_target_pairs={{0,6},{1,7},{2,4},{3,5},{4,2},{5,3},{6,0},{7,1}} | collective-permute-start | bytes 12296 | tf_op jit(solution)/shard_map/ppermute | solution.py:355
  54.8 4.3 collective-permute-start.16
  55.1 5.0 collective-permute-start.15
  57.9 4.0 collective-permute-start.18
  59.1 105.6 %collective-permute-start.7 = (bf16[256,4096]{1,0:T(8,128)(2,1)}, bf16[256,4096]{1,0:T(8,128)(2,1)}, u32[]{:S(2)}, u32[]{:S(2)}) collective-permute-start(bf16[256,4096]{1,0:T(8,128)(2,1)} %refs_1_.2), channel_id=1, source_target_pairs={{0,4},{1,5},{2,6},{3,7},{4,0},{5,1},{6,2},{7,3}} | collective-permute-start | bytes 6291464 | tf_op jit(solution)/shard_map/ppermute | solution.py:355
  60.2 104.5 %collective-permute-start.6 = (bf16[256,4096]{1,0:T(8,128)(2,1)}, bf16[256,4096]{1,0:T(8,128)(2,1)}, u32[]{:S(2)}, u32[]{:S(2)}) collective-permute-start(bf16[256,4096]{1,0:T(8,128)(2,1)} %refs_1_.2), channel_id=1, source_target_pairs={{0,2},{1,3},{2,0},{3,1},{4,6},{5,7},{6,4},{7,5}} | collective-permute-start | bytes 6291464 | tf_op jit(solution)/shard_map/ppermute | solution.py:355
  61.9 47.6 %collective-permute-start.14 = (f32[16,256]{1,0:T(8,128)S(1)}, f32[16,256]{1,0:T(8,128)S(1)}, u32[]{:S(2)}, u32[]{:S(2)}) collective-permute-start(f32[16,256]{1,0:T(8,128)S(1)} %bitcast.81), channel_id=1, source_target_pairs={{0,7},{1,6},{2,5},{3,4},{4,3},{5,2},{6,1},{7,0}} | collective-permute-start | bytes 49160 | tf_op jit(solution)/shard_map/ppermute | solution.py:355
  109.4 14.3 %collective-permute-start.13 = (f32[16,256]{1,0:T(8,128)S(1)}, f32[16,256]{1,0:T(8,128)S(1)}, u32[]{:S(2)}, u32[]{:S(2)}) collective-permute-start(f32[16,256]{1,0:T(8,128)S(1)} %bitcast.82), channel_id=1, source_target_pairs={{0,6},{1,7},{2,4},{3,5},{4,2},{5,3},{6,0},{7,1}} | collective-permute-start | bytes 49160 | tf_op jit(solution)/shard_map/ppermute | solution.py:355
  110.1 14.2 %collective-permute-start.12 = (f32[16,256]{1,0:T(8,128)S(1)}, f32[16,256]{1,0:T(8,128)S(1)}, u32[]{:S(2)}, u32[]{:S(2)}) collective-permute-start(f32[16,256]{1,0:T(8,128)S(1)} %bitcast.83), channel_id=1, source_target_pairs={{0,5},{1,4},{2,7},{3,6},{4,1},{5,0},{6,3},{7,2}} | collective-permute-start | bytes 49160 | tf_op jit(solution)/shard_map/ppermute | solution.py:355
  110.7 14.6 %collective-permute-start.11 = (f32[16,256]{1,0:T(8,128)S(1)}, f32[16,256]{1,0:T(8,128)S(1)}, u32[]{:S(2)}, u32[]{:S(2)}) collective-permute-start(f32[16,256]{1,0:T(8,128)S(1)} %bitcast.84), channel_id=1, source_target_pairs={{0,4},{1,5},{2,6},{3,7},{4,0},{5,1},{6,2},{7,3}} | collective-permute-start | bytes 49160 | tf_op jit(solution)/shard_map/ppermute | solution.py:355
  123.8 40.7 %collective-permute-start.10 = (f32[16,256]{1,0:T(8,128)S(1)}, f32[16,256]{1,0:T(8,128)S(1)}, u32[]{:S(2)}, u32[]{:S(2)}) collective-permute-start(f32[16,256]{1,0:T(8,128)S(1)} %bitcast.85), channel_id=1, source_target_pairs={{0,3},{1,2},{2,1},{3,0},{4,7},{5,6},{6,5},{7,4}} | collective-permute-start | bytes 49160 | tf_op jit(solution)/shard_map/ppermute | solution.py:355
  124.4 40.4 %collective-permute-start.9 = (f32[16,256]{1,0:T(8,128)S(1)}, f32[16,256]{1,0:T(8,128)S(1)}, u32[]{:S(2)}, u32[]{:S(2)}) collective-permute-start(f32[16,256]{1,0:T(8,128)S(1)} %bitcast.86), channel_id=1, source_target_pairs={{0,2},{1,3},{2,0},{3,1},{4,6},{5,7},{6,4},{7,5}} | collective-permute-start | bytes 49160 | tf_op jit(solution)/shard_map/ppermute | solution.py:355
  125.3 39.4 %collective-permute-start.8 = (f32[16,256]{1,0:T(8,128)S(1)}, f32[16,256]{1,0:T(8,128)S(1)}, u32[]{:S(2)}, u32[]{:S(2)}) collective-permute-start(f32[16,256]{1,0:T(8,128)S(1)} %bitcast.87), channel_id=1, source_target_pairs={{0,1},{1,0},{2,3},{3,2},{4,5},{5,4},{6,7},{7,6}} | collective-permute-start | bytes 49160 | tf_op jit(solution)/shard_map/ppermute | solution.py:355
  164.5 5.7 %collective-permute-start.19 = (bf16[256,4096]{1,0:T(8,128)(2,1)}, bf16[256,4096]{1,0:T(8,128)(2,1)}, u32[]{:S(2)}, u32[]{:S(2)}) collective-permute-start(bf16[256,4096]{1,0:T(8,128)(2,1)} %refs_1_.2), channel_id=1, source_target_pairs={{0,1},{1,0},{2,3},{3,2},{4,5},{5,4},{6,7},{7,6}} | collective-permute-start | bytes 6291464 | tf_op jit(solution)/shard_map/ppermute | solution.py:355
  164.7 7.3 %collective-permute-start.20 = (bf16[256,4096]{1,0:T(8,128)(2,1)}, bf16[256,4096]{1,0:T(8,128)(2,1)}, u32[]{:S(2)}, u32[]{:S(2)}) collective-permute-start(bf16[256,4096]{1,0:T(8,128)(2,1)} %collective-permute-done.6.refs_3_), channel_id=1, source_target_pairs={{0,1},{1,0},{2,3},{3,2},{4,5},{5,4},{6,7},{7,6}} | collective-permute-start | bytes 6291464 | tf_op jit(solution)/shard_map/ppermute | solution.py:355
  168.3 110.0 %collective-permute-start.21 = (bf16[256,4096]{1,0:T(8,128)(2,1)}, bf16[256,4096]{1,0:T(8,128)(2,1)}, u32[]{:S(2)}, u32[]{:S(2)}) collective-permute-start(bf16[256,4096]{1,0:T(8,128)(2,1)} %copy-done.2), channel_id=1, source_target_pairs={{0,4},{1,5},{2,6},{3,7},{4,0},{5,1},{6,2},{7,3}} | collective-permute-start | bytes 6291464 | tf_op jit(solution)/shard_map/ppermute | solution.py:355
  272.0 58.3 %collective-permute-start.29 = (f32[256,4096]{1,0:T(8,128)}, f32[256,4096]{1,0:T(8,128)}, u32[]{:S(2)}, u32[]{:S(2)}) collective-permute-start(f32[256,4096]{1,0:T(8,128)} %get-tuple-element.80), channel_id=1, source_target_pairs={{0,1},{1,0},{2,3},{3,2},{4,5},{5,4},{6,7},{7,6}} | collective-permute-start | bytes 12582920 | tf_op jit(solution)/shard_map/ppermute | solution.py:355
  272.2 48.0 %collective-permute-start.26 = (bf16[256,4096]{1,0:T(8,128)(2,1)}, bf16[256,4096]{1,0:T(8,128)(2,1)S(1)}, u32[]{:S(2)}, u32[]{:S(2)}) collective-permute-start(bf16[256,4096]{1,0:T(8,128)(2,1)} %refs_0_.1), channel_id=1, source_target_pairs={{0,4},{1,5},{2,6},{3,7},{4,0},{5,1},{6,2},{7,3}} | collective-permute-start | bytes 6291464 | tf_op jit(solution)/shard_map/ppermute | solution.py:355
  276.2 3.1 collective-permute-start.24
  277.7 3.6 collective-permute-start.23
  278.3 3.0 collective-permute-start.22
  281.3 55.1 %collective-permute-start.28 = (bf16[256,4096]{1,0:T(8,128)(2,1)}, bf16[256,4096]{1,0:T(8,128)(2,1)}, u32[]{:S(2)}, u32[]{:S(2)}) collective-permute-start(bf16[256,4096]{1,0:T(8,128)(2,1)} %collective-permute-done.21.refs_2_), channel_id=1, source_target_pairs={{0,1},{1,0},{2,3},{3,2},{4,5},{5,4},{6,7},{7,6}} | collective-permute-start | bytes 6291464 | tf_op jit(solution)/shard_map/ppermute | solution.py:355
  320.3 16.1 %copy-start.3 = (bf16[256,4096]{1,0:T(8,128)(2,1)}, bf16[256,4096]{1,0:T(8,128)(2,1)S(1)}, u32[]{:S(2)}) copy-start(bf16[256,4096]{1,0:T(8,128)(2,1)S(1)} %collective-permute-done.26.refs_0_) | copy-start | bytes 6291460
  320.3 16.4 %collective-permute-start.27 = (bf16[256,4096]{1,0:T(8,128)(2,1)S(1)}, bf16[256,4096]{1,0:T(8,128)(2,1)}, u32[]{:S(2)}, u32[]{:S(2)}) collective-permute-start(bf16[256,4096]{1,0:T(8,128)(2,1)S(1)} %collective-permute-done.26.refs_0_), channel_id=1, source_target_pairs={{0,1},{1,0},{2,3},{3,2},{4,5},{5,4},{6,7},{7,6}} | collective-permute-start | bytes 6291464 | tf_op jit(solution)/shard_map/ppermute | solution.py:355
  320.3 67.2 %collective-permute-start.31 = (bf16[256,4096]{1,0:T(8,128)(2,1)}, bf16[256,4096]{1,0:T(8,128)(2,1)}, u32[]{:S(2)}, u32[]{:S(2)}) collective-permute-start(bf16[256,4096]{1,0:T(8,128)(2,1)} %collective-permute-done.6.refs_3_), channel_id=1, source_target_pairs={{0,4},{1,5},{2,6},{3,7},{4,0},{5,1},{6,2},{7,3}} | collective-permute-start | bytes 6291464 | tf_op jit(solution)/shard_map/ppermute | solution.py:355
  324.3 66.8 %collective-permute-start.30 = (bf16[256,4096]{1,0:T(8,128)(2,1)}, bf16[256,4096]{1,0:T(8,128)(2,1)}, u32[]{:S(2)}, u32[]{:S(2)}) collective-permute-start(bf16[256,4096]{1,0:T(8,128)(2,1)} %collective-permute-done.7.refs_1_), channel_id=1, source_target_pairs={{0,1},{1,0},{2,3},{3,2},{4,5},{5,4},{6,7},{7,6}} | collective-permute-start | bytes 6291464 | tf_op jit(solution)/shard_map/ppermute | solution.py:355
  336.4 51.1 %collective-permute-start.32 = (f32[16,4096]{1,0:T(8,128)S(1)}, f32[16,4096]{1,0:T(8,128)S(1)}, u32[]{:S(2)}, u32[]{:S(2)}) collective-permute-start(f32[16,4096]{1,0:T(8,128)S(1)} %fusion.17), channel_id=1, source_target_pairs={{0,1},{1,0},{2,3},{3,2},{4,5},{5,4},{6,7},{7,6}} | collective-permute-start | bytes 786440 | tf_op jit(solution)/shard_map/ppermute | solution.py:355
  387.5 4.5 collective-permute-start.33
  388.3 131.0 %collective-permute-start.25 = (f32[256,4096]{1,0:T(8,128)}, f32[256,4096]{1,0:T(8,128)}, u32[]{:S(2)}, u32[]{:S(2)}) collective-permute-start(f32[256,4096]{1,0:T(8,128)} %get-tuple-element.76), channel_id=1, source_target_pairs={{0,1},{1,0},{2,3},{3,2},{4,5},{5,4},{6,7},{7,6}} | collective-permute-start | bytes 12582920 | tf_op jit(solution)/shard_map/ppermute | solution.py:355
  388.6 129.3 %collective-permute-start.36 = (f32[256,4096]{1,0:T(8,128)}, f32[256,4096]{1,0:T(8,128)}, u32[]{:S(2)}, u32[]{:S(2)}) collective-permute-start(f32[256,4096]{1,0:T(8,128)} %add.116), channel_id=1, source_target_pairs={{0,2},{1,3},{2,0},{3,1},{4,6},{5,7},{6,4},{7,5}} | collective-permute-start | bytes 12582920 | tf_op jit(solution)/shard_map/ppermute | solution.py:355
  390.6 41.1 %collective-permute-start.34 = (f32[16,4096]{1,0:T(8,128)S(1)}, f32[16,4096]{1,0:T(8,128)S(1)}, u32[]{:S(2)}, u32[]{:S(2)}) collective-permute-start(f32[16,4096]{1,0:T(8,128)S(1)} %add.119), channel_id=1, source_target_pairs={{0,4},{1,5},{2,6},{3,7},{4,0},{5,1},{6,2},{7,3}} | collective-permute-start | bytes 786440 | tf_op jit(solution)/shard_map/ppermute | solution.py:355
  431.7 86.1 %collective-permute-start.35 = (f32[16,4096]{1,0:T(8,128)S(1)}, f32[16,4096]{1,0:T(8,128)S(1)}, u32[]{:S(2)}, u32[]{:S(2)}) collective-permute-start(f32[16,4096]{1,0:T(8,128)S(1)} %add.120), channel_id=1, source_target_pairs={{0,2},{1,3},{2,0},{3,1},{4,6},{5,7},{6,4},{7,5}} | collective-permute-start | bytes 786440 | tf_op jit(solution)/shard_map/ppermute | solution.py:355
  517.9 2.3 copy-start.1
where the time goes:
time: 528 us; the launch traced here: 526 us
  Pallas kernels  325 us (62%)
  waiting for transfers between devices  127 us (24%)
  starting transfers between devices  28.9 us (5%)
  other arithmetic  23.9 us (5%)
  local copies, waits for them, and re-layouts  10.1 us (2%)
  between operations  6.04 us (1%)
    pallas_call x4, Pallas kernels, tile_kernel_call(): pl.pallas_call(functools.partial(kernel, n_c), grid_spec=pltpu.PrefetchSc...  145 us
    ppermute x37, waiting for transfers between devices, shift(): return lax.ppermute(arr, axes, pairs)  127 us
    pallas_call x1, Pallas kernels, wgrad(): pl.pallas_call(wgrad_kernel, grid_spec=pltpu.PrefetchScalarGridSpec(num_s...  84.1 us
    pallas_call x4, Pallas kernels, dispatch(): pl.pallas_call(functools.partial(dispatch_kernel, with_g, gated), grid=(d...  49.2 us
    pallas_call x1, Pallas kernels, back(): pl.pallas_call(back_kernel, grid_spec=pltpu.PrefetchScalarGridSpec(num_sc...  46.6 us
    ppermute x37, starting transfers between devices, shift(): return lax.ppermute(arr, axes, pairs)  28.9 us
  transfers between devices with their start and end apart: 37, of which 8 were waited for; matrix products, arithmetic and copies ran while one was open for 6% of the time, Pallas kernels for 62%

commit v1 on v0

--- a/solution.py
+++ b/solution.py
@@ -30,164 +30,201 @@
     return pl.CostEstimate(flops=int(flops), bytes_accessed=int(nbytes), transcendentals=0)
 
 
-def dispatch_kernel(with_g, gated, slots, *refs):
-    if gated:
-        gates, v, refs = refs[0], refs[1:5], refs[5:]
-        do_out, g_out = refs[0], (refs[1] if with_g else None)
-        sel, col = refs[-2:]
-    else:
-        v, (x_out, sel) = refs[0:4], refs[4:]
-
-    @pl.when(pl.program_id(0) == 0)
+def expert_kernel(mode, n_c, dc, ring, eidx, act, slots, gates, *refs):
+    has_x, has_g = mode != "grad", mode != "fwd"
+    it = iter(refs)
+
+    def take(n):
+        return [next(it) for _ in range(n)]
+
+    xs, gs = take(4 * has_x), take(4 * has_g)
+    n_w = {"fwd": 2, "grad": 1, "both": 3}[mode]
+    w_hbm = take(n_w)
+    z_hbm = take(2) if mode == "grad" else []
+    x_out, do_out = take(1 * has_x), take(1 * has_g)
+    if mode == "fwd":
+        z_hbm = take(2)
+    hid, more = take(3 * has_g), take(3 * (mode == "grad"))
+    acc = take(3 if mode == "both" else 2)
+    zs = take(2 * (mode == "grad"))
+    g_sc = take(1 * (mode == "grad"))
+    wbuf, wsem = take(2)
+    zsem = take(1 * (mode != "both"))
+    c = pl.program_id(0)
+
+    def w_copies(f, expert, slot):
+        cols = pl.ds(pl.multiple_of((f // 4) * dc, dc), dc)
+        return [pltpu.make_async_copy(w_hbm[n].at[expert, :, cols], wbuf.at[slot, n], wsem.at[slot, n])
+                for n in range(n_w)]
+
+    def ring_copies(f):
+        return w_copies(f, eidx[lax.rem(f, 4)], lax.rem(f, ring))
+
+    def z_copies(i):
+        if mode == "fwd":
+            return [pltpu.make_async_copy(acc[n].at[i], z_hbm[n].at[i], zsem[0].at[n, i]) for n in range(2)]
+        return [pltpu.make_async_copy(z_hbm[n].at[i], zs[n].at[i], zsem[0].at[n, i]) for n in range(2)]
+
+    def each_active(fn):
+        for i in range(8):
+            @pl.when(act[i] == 1)
+            def _():
+                fn(i)
+
+    @pl.when(c == 0)
     def _():
-        for k in range(4):
-            for m in range(5):
-                n = OVER if m == 4 else COLD
-                lo = COLD * m
-                row = lax.broadcasted_iota(jnp.int32, (n, 256), 0).astype(F32) + float(lo)
-                hit = slots[k, m:m + 1, :] == row
-                sel[k, lo:lo + n, :] = jnp.where(hit, 1.0, 0.0).astype(BF16)
-                if gated:
-                    col[k, lo:lo + n, :] = jnp.sum(jnp.where(hit, gates[k, m:m + 1, :], 0.0), axis=1, keepdims=True)
-
-    def put(out, k, rows):
-        for j in range(4):
-            out[j, COLD * k:COLD * (k + 1), :] = rows[COLD * j:COLD * (j + 1)]
-        out[4 + k // 2, OVER * (k % 2):OVER * (k % 2) + OVER, :] = rows[256:384]
-
-    for k in range(4):
-        rows = mm(sel[k], v[k][...], NN)
-        if gated:
-            put(do_out, k, (col[k] * rows).astype(BF16))
-            if with_g:
-                put(g_out, k, rows.astype(BF16))
+        for f in range(ring - 1):
+            for copy in ring_copies(jnp.int32(f)):
+                copy.start()
+        if mode == "grad":
+            each_active(lambda i: [copy.start() for copy in z_copies(i)])
+
+    def gather(k, row, gate, base, n, tile, lo):
+        want = lax.broadcasted_iota(jnp.int32, (n, 256), 0) + base
+        hit = row == want.astype(F32)
+        sel = jnp.where(hit, 1.0, 0.0).astype(BF16)
+        if has_x:
+            x_out[0][tile, lo:lo + n, :] = mm(sel, xs[k][...], NN).astype(BF16)
+        if has_g:
+            rows = mm(sel, gs[k][...], NN)
+            col = jnp.sum(jnp.where(hit, gate, 0.0), axis=1, keepdims=True)
+            do_out[0][tile, lo:lo + n, :] = (col * rows).astype(BF16)
+            if mode == "grad":
+                g_sc[0][lo:lo + n, :] = rows.astype(BF16)
+
+    def finish(i, tile, lo):
+        n = 128
+        cols = slice(lo, lo + n)
+        if mode == "grad":
+            z_gate, z_up, d_act = zs[0][i, :, cols], zs[1][i, :, cols], acc[0][i, :, cols]
         else:
-            put(x_out, k, rows.astype(BF16))
-
-
-def dispatch(slots, gates, vs, with_g):
-    tok, dim = vs[0].shape
-    dc = 512
-    gated = gates is not None
-    small = pl.BlockSpec((4, 8, 256), lambda c: (0, 0, 0))
-    n_out = 2 if with_g else 1
-    scratch = [pltpu.VMEM((4, 384, 256), BF16)]
-    if gated:
-        scratch.append(pltpu.VMEM((4, 384, 1), F32))
-    return pl.pallas_call(
-        functools.partial(dispatch_kernel, with_g, gated),
-        grid=(dim // dc,),
-        in_specs=[small] * (2 if gated else 1) + [pl.BlockSpec((tok, dc), lambda c: (0, c))] * 4,
-        out_specs=[pl.BlockSpec((6, 256, dc), lambda c: (0, 0, c))] * n_out,
-        out_shape=[jax.ShapeDtypeStruct((6, 256, dim), BF16)] * n_out,
-        scratch_shapes=scratch,
-        compiler_params=pltpu.CompilerParams(vmem_limit_bytes=VMEM_LIMIT),
-        cost_estimate=cost(2 * 1536 * 256 * dim, 2 * n_out * 1536 * dim * 2),
-        name="dispatch",
-    )(*([slots, gates] if gated else [slots]), *vs)
-
-
-def tile_kernel_call(kernel, eidx, act, rows, weights, late, outs, n_mm):
-    ff, dim = weights[0].shape[1:]
-    dc = 2048
-    n_c = dim // dc
-
-    def last(c, i, e):
-        return jnp.where(c == n_c - 1, tile_of(i, e), tile_of(0, e))
-
-    row_blk = pl.BlockSpec((1, 256, dc), lambda c, i, e, t: (tile_of(i, e), 0, c))
-    w_blk = pl.BlockSpec((1, ff, dc), lambda c, i, e, t: (e[i], 0, c))
-    late_blk = pl.BlockSpec((1, ff, 256), lambda c, i, e, t: (last(c, i, e), 0, 0))
-    return pl.pallas_call(
-        functools.partial(kernel, n_c),
-        grid_spec=pltpu.PrefetchScalarGridSpec(
-            num_scalar_prefetch=2, grid=(n_c, 8),
-            in_specs=[row_blk] * len(rows) + [w_blk] * len(weights) + [late_blk] * len(late),
-            out_specs=[pl.BlockSpec((1,) + o.shape[1:], lambda c, i, e, t: (last(c, i, e), 0, 0)) for o in outs],
-            scratch_shapes=[pltpu.VMEM((8, ff, 256), F32)] * n_mm),
-        out_shape=outs,
-        compiler_params=pltpu.CompilerParams(vmem_limit_bytes=VMEM_LIMIT),
-        cost_estimate=cost(n_mm * 2 * 1536 * dim * ff, 80e6),
-    )(eidx, act, *rows, *weights, *late)
-
-
-def accumulate(act, acc, terms, n_c, finish):
-    c, step = pl.program_id(0), pl.program_id(1)
-
-    @pl.when(act[step] == 1)
-    def _():
-        for ref, val in zip(acc, terms()):
-            ref[step] = jnp.where(c == 0, 0.0, ref[step]) + val
-
-    @pl.when((act[step] == 1) & (c == n_c - 1))
-    def _():
-        @pl.when((step != 5) & (step != 7))
-        def _():
-            finish(step, 0)
-
-        finish(step, 128)
-
-
-def forward_kernel(n_c, eidx, act, x, w1, w3, s_out, zu_out, sp_out, a_out, z1, z3):
-    def terms():
-        yield mm(w1[0], x[0], NT)
-        yield mm(w3[0], x[0], NT)
-
-    def finish(step, lo):
-        n = 128
-        z_gate, z_up = z1[step, :, lo:lo + n], z3[step, :, lo:lo + n]
+            z_gate, z_up, d_act = acc[0][i, :, cols], acc[1][i, :, cols], acc[2][i, :, cols]
         sig = jax.nn.sigmoid(z_gate)
         silu = z_gate * sig
-        s_out[0, :, lo:lo + n] = silu
-        zu_out[0, :, lo:lo + n] = z_up
-        sp_out[0, :, lo:lo + n] = sig * (1.0 + z_gate * (1.0 - sig))
-        a_out[0, :, lo:lo + n] = (silu * z_up).astype(BF16)
-
-    accumulate(act, (z1, z3), terms, n_c, finish)
-
-
-def hidden_grad_kernel(with_g, n_c, eidx, act, *refs):
-    if with_g:
-        do, g, w2, s_in, zu_in, sp_in, a_in, d1_out, d3_out, q_out, d1r_out, d3r_out, da, hg = refs
-    else:
-        do, w2, s_in, zu_in, sp_in, d1_out, d3_out, da = refs
-
-    def terms():
-        yield mm(w2[0], do[0], NT)
-        if with_g:
-            yield mm(w2[0], g[0], NT)
-
-    def finish(step, lo):
-        n = 128
-        d_act = da[step, :, lo:lo + n]
-        d1 = (d_act * zu_in[0, :, lo:lo + n] * sp_in[0, :, lo:lo + n]).astype(BF16)
-        d3 = (d_act * s_in[0, :, lo:lo + n]).astype(BF16)
-        d1_out[0, :, lo:lo + n] = d1
-        d3_out[0, :, lo:lo + n] = d3
-        if with_g:
-            a = a_in[0, :, lo:lo + n].astype(F32)
-            q = jnp.sum(a * hg[step, :, lo:lo + n], axis=0, keepdims=True)
-            q_out[0, :, lo:lo + n] = jnp.broadcast_to(q, (8, n))
-            d1r_out[0, lo:lo + n, :] = d1.astype(F32).T.astype(BF16)
-            d3r_out[0, lo:lo + n, :] = d3.astype(F32).T.astype(BF16)
-
-    accumulate(act, (da, hg) if with_g else (da,), terms, n_c, finish)
-
-
-def forward(eidx, act, x, w1t, w3t):
-    ff = w1t.shape[1]
-    outs = [jax.ShapeDtypeStruct((6, ff, 256), F32)] * 3 + [jax.ShapeDtypeStruct((6, ff, 256), BF16)]
-    return tile_kernel_call(forward_kernel, eidx, act, [x], [w1t, w3t], [], outs, 2)
-
-
-def hidden_grad(eidx, act, rows, w2, late):
-    ff = w2.shape[1]
-    with_g = len(rows) == 2
-    outs = [jax.ShapeDtypeStruct((6, ff, 256), BF16)] * 2
-    if with_g:
-        outs += [jax.ShapeDtypeStruct((6, 8, 256), F32)] + [jax.ShapeDtypeStruct((6, 256, ff), BF16)] * 2
-    kernel = functools.partial(hidden_grad_kernel, with_g)
-    return tile_kernel_call(kernel, eidx, act, rows, [w2], late, outs, len(rows))
+        a = (silu * z_up).astype(BF16)
+        d1 = (d_act * z_up * sig * (1.0 + z_gate * (1.0 - sig))).astype(BF16)
+        d3 = (d_act * silu).astype(BF16)
+        for out, val in zip(hid, (a, d1, d3)):
+            out[tile, :, cols] = val
+        if mode == "grad":
+            q_out, d1r_out, d3r_out = more
+            q = jnp.sum(a.astype(F32) * acc[1][i, :, cols], axis=0, keepdims=True)
+            q_out[tile, :, cols] = jnp.broadcast_to(q, (8, n))
+            d1r_out[tile, cols, :] = d1.astype(F32).T.astype(BF16)
+            d3r_out[tile, cols, :] = d3.astype(F32).T.astype(BF16)
+
+    def step(i, _):
+        expert = eidx[i]
+        tile = tile_of(i, eidx)
+        f = c * 4 + jnp.minimum(i, 3)
+        stray = (i >= 4) & (expert != eidx[3])
+        slot = jnp.where(stray, ring, lax.rem(f, ring))
+
+        @pl.when(i < 4)
+        def _():
+            @pl.when(f + ring - 1 < 4 * n_c)
+            def _():
+                for copy in ring_copies(f + ring - 1):
+                    copy.start()
+
+            for k in range(4):
+                gather(k, slots[k, pl.ds(expert, 1), :], gates[k, pl.ds(expert, 1), :], expert * COLD, COLD, tile, COLD * k)
+            for copy in ring_copies(f):
+                copy.wait()
+
+        for q in range(2):
+            @pl.when(i == 4 + 2 * q)
+            def _():
+                for half in range(2):
+                    k = 2 * q + half
+                    gather(k, slots[k, 4:5, :], gates[k, 4:5, :], 4 * COLD, OVER, 4 + q, OVER * half)
+
+        @pl.when((act[i] == 1) & stray)
+        def _():
+            for copy in w_copies(f, expert, ring):
+                copy.start()
+            for copy in w_copies(f, expert, ring):
+                copy.wait()
+
+        @pl.when(act[i] == 1)
+        def _():
+            def add(ref, val):
+                ref[i] = jnp.where(c == 0, 0.0, ref[i]) + val
+
+            if has_x:
+                x = x_out[0][tile]
+                add(acc[0], mm(wbuf[slot, 0], x, NT))
+                add(acc[1], mm(wbuf[slot, 1], x, NT))
+            if has_g:
+                add(acc[0 if mode == "grad" else 2], mm(wbuf[slot, n_w - 1], do_out[0][tile], NT))
+            if mode == "grad":
+                add(acc[1], mm(wbuf[slot, 0], g_sc[0][...], NT))
+
+        @pl.when((act[i] == 1) & (c == n_c - 1))
+        def _():
+            if mode == "fwd":
+                for copy in z_copies(i):
+                    copy.start()
+            else:
+                if mode == "grad":
+                    for copy in z_copies(i):
+                        copy.wait()
+
+                @pl.when((i != 5) & (i != 7))
+                def _():
+                    finish(i, tile, 0)
+
+                finish(i, tile, 128)
+
+        return 0
+
+    lax.fori_loop(0, 8, step, 0)
+
+    if mode == "fwd":
+        @pl.when(c == n_c - 1)
+        def _():
+            each_active(lambda i: [copy.wait() for copy in z_copies(i)])
+
+
+def experts(mode, eidx, act, slots, gates, xs, gs, weights, zs, dc, ring):
+    has_x, has_g = mode != "grad", mode != "fwd"
+    ff, dim = weights[0].shape[1:]
+    n_c = dim // dc
+    any_blk = pl.BlockSpec(memory_space=pl.ANY)
+    small = pl.BlockSpec((4, 8, 256), lambda c, e, t: (0, 0, 0))
+    v_blk = pl.BlockSpec((256, dc), lambda c, e, t: (0, c))
+
+    def whole(d0, d1, dtype):
+        return (jax.ShapeDtypeStruct((6, d0, d1), dtype),
+                pl.BlockSpec((6, d0, d1), lambda c, e, t: (0, 0, 0), pipeline_mode=pl.Buffered(1)))
+
+    outs = [(jax.ShapeDtypeStruct((6, 256, dim), BF16),
+             pl.BlockSpec((6, 256, dc), lambda c, e, t: (0, 0, c)))] * (has_x + has_g)
+    if mode == "fwd":
+        outs += [(jax.ShapeDtypeStruct((8, ff, 256), F32), any_blk)] * 2
+    if has_g:
+        outs += [whole(ff, 256, BF16)] * 3
+    if mode == "grad":
+        outs += [whole(8, 256, F32), whole(256, ff, BF16), whole(256, ff, BF16)]
+    n_acc = 3 if mode == "both" else 2
+    scratch = [pltpu.VMEM((8, ff, 256), F32)] * (n_acc + len(zs))
+    if mode == "grad":
+        scratch.append(pltpu.VMEM((256, dc), BF16))
+    scratch += [pltpu.VMEM((ring + 1, len(weights), ff, dc), BF16), pltpu.SemaphoreType.DMA((ring + 1, len(weights)))]
+    if mode != "both":
+        scratch.append(pltpu.SemaphoreType.DMA((2, 8)))
+    n_v = len(xs) + len(gs)
+    n_mm = 4 if mode == "both" else 2
+    return pl.pallas_call(
+        functools.partial(expert_kernel, mode, n_c, dc, ring),
+        grid_spec=pltpu.PrefetchScalarGridSpec(
+            num_scalar_prefetch=2, grid=(n_c,),
+            in_specs=[small] * 2 + [v_blk] * n_v + [any_blk] * (len(weights) + len(zs)),
+            out_specs=[o[1] for o in outs], scratch_shapes=scratch),
+        out_shape=[o[0] for o in outs],
+        compiler_params=pltpu.CompilerParams(vmem_limit_bytes=VMEM_LIMIT),
+        cost_estimate=cost(n_mm * 2 * 1536 * dim * ff, 90e6),
+    )(eidx, act, slots, gates, *xs, *gs, *weights, *zs)
 
 
 def back_kernel(eidx, act, d1, d3, w1, w3, s0, s1, s2, s3, o0, o1, o2, o3, r_sc):
@@ -410,15 +447,17 @@
         x_across_sib = shift(x_across, 0, 1)
         x_ya = shift(x_across, 1, 0)
         x_ys = shift(x_y, 0, 1)
-        xa, = dispatch(slots_a, None, (x_loc, x_sib, x_across, x_across_sib), False)
-        s_a, zu_a, sp_a, a_a = forward(eidx_a, act_a, xa, w1t, w3t)
-        a_a, g_across, g_y, gates_a, gates_b, idx_b = lax.optimization_barrier((a_a, g_across, g_y, gates_a, gates_b, idx_b))
+        gate_a0 = jnp.zeros((4, 8, tok), F32)
+        xa, z1_a, z3_a = experts("fwd", eidx_a, act_a, slots_a, gate_a0, (x_loc, x_sib, x_across, x_across_sib), (),
+                                 (w1t, w3t), (), 1024, 4)
+        z1_a, g_across, g_y, gates_a, gates_b, idx_b = lax.optimization_barrier((z1_a, g_across, g_y, gates_a, gates_b, idx_b))
         ranks_b, slots_b, hot_b, eidx_b, act_b = tables(idx_b)
         g_across_sib = shift(g_across, 0, 1)
         g_ya = shift(g_across, 1, 0)
         g_ys = shift(g_y, 0, 1)
-        da, ga = dispatch(slots_a, gate_table(gates_a, ranks_a), (dy_loc, g_sib, g_across, g_across_sib), True)
-        d1_a, d3_a, q_a, d1r_a, d3r_a = hidden_grad(eidx_a, act_a, (da, ga), w2, (s_a, zu_a, sp_a, a_a))
+        gate_a = gate_table(gates_a, ranks_a)
+        da, a_a, d1_a, d3_a, q_a, d1r_a, d3r_a = experts(
+            "grad", eidx_a, act_a, slots_a, gate_a, (), (dy_loc, g_sib, g_across, g_across_sib), (w2,), (z1_a, z3_a), 1024, 4)
         slots_t = jnp.swapaxes(slots_a, 1, 2)
         part = back(eidx_a, act_a, d1r_a, d3r_a, w1t, w3t, [slots_t[k] for k in range(4)])
 
@@ -431,8 +470,10 @@
         q_tok = q_tok + jnp.sum(jnp.where(ranks_a[..., None] == r128, q_over[:, None, None, :], 0.0), axis=3)
         q_recv = [shift(q_tok[k], 0, k) for k in (1, 2, 3)]
 
-        part_own, x_ya, q_recv = lax.optimization_barrier((part[0], x_ya, q_recv))
+        part_own, x_ya, g_ya, q_recv = lax.optimization_barrier((part[0], x_ya, g_ya, q_recv))
         x_yas = shift(x_ya, 0, 1)
+        g_yas = shift(g_ya, 0, 1)
+        gate_b = gate_table(gates_b, ranks_b)
 
         to_sib = shift(part[1], 0, 1)
         pair = part[2] + shift(part[3], 0, 1)
@@ -443,17 +484,13 @@
         d_logits = d_sel.astype(BF16)
         gr = jnp.dot(d_logits, x_loc, preferred_element_type=F32)
 
-        x_yas, pair, gr = lax.optimization_barrier((x_yas, pair, gr))
+        x_yas, g_yas, pair, gr = lax.optimization_barrier((x_yas, g_yas, pair, gr))
         from_across = shift(pair, 0, 2)
-        gr_recv = shift(gr, 0, 1)
-        xb, = dispatch(slots_b, None, (x_y, x_ys, x_ya, x_yas), False)
-        s_b, zu_b, sp_b, a_b = forward(eidx_b, act_b, xb, w1t, w3t)
-        a_b, s_b, g_ya, gr_recv = lax.optimization_barrier((a_b, s_b, g_ya, gr_recv))
-        g_yas = shift(g_ya, 0, 1)
-        gr = gr + gr_recv
+        gr = gr + shift(gr, 0, 1)
         gr_recv = shift(gr, 1, 0)
-        db, = dispatch(slots_b, gate_table(gates_b, ranks_b), (g_y, g_ys, g_ya, g_yas), False)
-        d1_b, d3_b = hidden_grad(eidx_b, act_b, (db,), w2, (s_b, zu_b, sp_b))
+        xb, db, a_b, d1_b, d3_b = experts(
+            "both", eidx_b, act_b, slots_b, gate_b, (x_y, x_ys, x_ya, x_yas), (g_y, g_ys, g_ya, g_yas),
+            (w1t, w3t, w2), (), 512, 4)
         d1_b, gr_recv = lax.optimization_barrier((d1_b, gr_recv))
         gr = gr + gr_recv
         gr_recv = shift(gr, 0, 2)

time: 528 us -> 499 us (0.945)
  Pallas kernels: 325 us -> 291 us
  waiting for transfers between devices: 127 us -> 137 us
    pallas_call x8 -> x3, Pallas kernels: 194 us -> 160 us  [experts(): pl.pallas_call(functools.partial(expert_kernel, mode, n_c, dc, ring), gri...]
    ppermute x37, waiting for transfers between devices: 127 us -> 137 us  [shift(): return lax.ppermute(arr, axes, pairs)]
  transfers between devices with their start and end apart: 37 -> 37, of which waited for: 8 -> 9; matrix products, arithmetic and copies ran while one was open for 6% -> 6% of each run, Pallas kernels for 62% -> 58%
where the time goes in v1:
time: 499 us; the launch traced here: 498 us
  Pallas kernels  291 us (58%)
  waiting for transfers between devices  137 us (27%)
  starting transfers between devices  28.2 us (6%)
  other arithmetic  21.6 us (4%)
  local copies, waits for them, and re-layouts  9.49 us (2%)
  between operations  6.07 us (1%)
  matrix products  5.27 us (1%)
    pallas_call x3, Pallas kernels, experts(): pl.pallas_call(functools.partial(expert_kernel, mode, n_c, dc, ring), gri...  160 us
    ppermute x37, waiting for transfers between devices, shift(): return lax.ppermute(arr, axes, pairs)  137 us
    pallas_call x1, Pallas kernels, wgrad(): pl.pallas_call(wgrad_kernel, grid_spec=pltpu.PrefetchScalarGridSpec(num_s...  84.1 us
    pallas_call x1, Pallas kernels, back(): pl.pallas_call(back_kernel, grid_spec=pltpu.PrefetchScalarGridSpec(num_sc...  46.7 us
    ppermute x37, starting transfers between devices, shift(): return lax.ppermute(arr, axes, pairs)  28.2 us
  transfers between devices with their start and end apart: 37, of which 9 were waited for; matrix products, arithmetic and copies ran while one was open for 6% of the time, Pallas kernels for 58%

profile of v1, /device:TPU:0, one launch (start us, length us, event | category | flops | bytes accessed | tf_op | source)
XLA Modules:
  0.0 498.2 jit_solution(17292877047219183173)
XLA Ops:
  0.7 3.3 collective-permute-start.4
  4.0 1.2 collective-permute-start.1
  5.2 0.7 collective-permute-start
  5.9 2.2 fusion.16
  8.2 41.9 %collective-permute-done.4.refs_2_ = bf16[256,4096]{1,0:T(8,128)(2,1)} collective-permute-done((bf16[256,4096]{1,0:T(8,128)(2,1)}, bf16[256,4096]{1,0:T(8,128)(2,1)}, u32[]{:S(2)}, u32[]{:S(2)}) %collective-permute-start.4) | collective-permute-done | bytes 2097184 | tf_op jit(solution)/shard_map/ppermute | solution.py:392
  50.2 2.7 collective-permute-start.17
  53.2 1.5 collective-permute-start.15
  55.2 1.2 collective-permute-start.18
  56.4 0.7 fusion.12
  57.5 1.4 collective-permute-start.6
  59.1 1.6 collective-permute-start.14
  60.8 46.5 %collective-permute-done.14 = f32[16,256]{1,0:T(8,128)S(1)} collective-permute-done((f32[16,256]{1,0:T(8,128)S(1)}, f32[16,256]{1,0:T(8,128)S(1)}, u32[]{:S(2)}, u32[]{:S(2)}) %collective-permute-start.14) | collective-permute-done | bytes 16416 | tf_op jit(solution)/shard_map/ppermute | solution.py:392
  108.0 4.0 collective-permute-done.13
  112.0 0.6 fusion.9
  112.7 2.5 collective-permute-done.12
  115.8 1.2 pad_add_fusion.2.eidx
  119.6 0.7 stack.99.act
  120.3 1.5 collective-permute-start.9
  122.8 40.8 %shard_map.110 = (bf16[6,256,4096]{2,1,0:T(8,128)(2,1)}, f32[8,688,256]{2,1,0:T(8,128)}, f32[8,688,256]{2,1,0:T(8,128)}) custom-call(s32[8]{0:T(128)} %pad_add_fusion.2.eidx, s32[8]{0:T(128)} %stack.99.act, f32[4,8,256]{2,1,0:T(8,128)} %get-tuple-element.115.slots, f32[4,8,256]{2,1,0:T(8,128)} %broadcast_in_dim.122.gates, bf16[256,4096]{1,0:T(8,128)(2,1)} %refs_0_.2, ...), custom_call_target="tpu_custom_call" | custom-call | flops 17314086912 | bytes 90000000 | tf_op jit(solution)/shard_map/pallas_call | solution.py:218
  164.3 0.8 copy.22.s3
  165.1 0.8 copy.21.s2
  165.8 0.8 copy.20.s1
  166.6 0.8 copy.19.s0
  167.4 1.4 collective-permute-start.21
  170.0 0.7 maximum_maximum_fusion.1
  171.1 49.0 %shard_map.111 = (bf16[6,256,4096]{2,1,0:T(8,128)(2,1)}, bf16[6,688,256]{2,1,0:T(8,128)(2,1)}, bf16[6,688,256]{2,1,0:T(8,128)(2,1)}, bf16[6,688,256]{2,1,0:T(8,1...) custom-call(s32[8]{0:T(128)} %pad_add_fusion.2.eidx, s32[8]{0:T(128)} %stack.99.act, ...), custom_call_target="tpu_custom_call" | custom-call | flops 17314086912 | bytes 90000000 | tf_op jit(solution)/shard_map/pallas_call | solution.py:218
  220.2 46.7 %back.1 = (f32[256,4096]{1,0:T(8,128)}, f32[256,4096]{1,0:T(8,128)}, f32[256,4096]{1,0:T(8,128)}, f32[256,4096]{1,0:T(8,128)}) custom-call(s32[8]{0:T(128)} %pad_add_fusion.2.eidx, s32[8]{0:T(128)} %stack.99.act, bf16[6,256,688]{2,1,0:T(8,128)(2,1)} %get-tuple-element.63.d1, bf16[6,256,688]{2,1,0:T(8,128)(2,1)} %get-tuple-element.64.d3, ...), custom_call_target="tpu_custom_call" | custom-call | flops 17314086912 | bytes 70000000 | tf_op jit(solution)/shard_map/back/pallas_call | solution.py:279
  267.1 1.4 collective-permute-start.27
  268.5 0.7 slice.72
  269.3 0.8 slice_reduce_fusion
  270.4 1.3 select_reduce_fusion
  271.8 1.5 collective-permute-start.24
  273.6 1.2 collective-permute-done.25
  274.8 0.7 collective-permute-done.24
  276.0 39.2 %collective-permute-done.27.refs_0_ = bf16[256,4096]{1,0:T(8,128)(2,1)} collective-permute-done((bf16[256,4096]{1,0:T(8,128)(2,1)}, bf16[256,4096]{1,0:T(8,128)(2,1)}, u32[]{:S(2)}, u32[]{:S(2)}) %collective-permute-start.27) | collective-permute-done | bytes 2097184 | tf_op jit(solution)/shard_map/ppermute | solution.py:392
  316.4 0.7 fusion.14
  318.3 2.0 fusion.17
  320.2 6.0 %add.117 = f32[256,4096]{1,0:T(8,128)} add(f32[256,4096]{1,0:T(8,128)} %get-tuple-element.77, f32[256,4096]{1,0:T(8,128)} %collective-permute-done.31) | non-fusion elementwise | flops 1048576 | bytes 12582912 | tf_op jit(solution)/shard_map/add | solution.py:479
  326.3 1.1 pad_add_fusion.4.eidx
  330.6 0.7 maximum_maximum_fusion.2.slots
  332.1 1.7 collective-permute-start.34
  333.8 70.3 %shard_map.112 = (bf16[6,256,4096]{2,1,0:T(8,128)(2,1)}, bf16[6,256,4096]{2,1,0:T(8,128)(2,1)}, bf16[6,688,256]{2,1,0:T(8,128)(2,1)}, bf16[6,688,256]{2,1,0:T(8,128)(2,1)}, bf16[6,688,256]{2,1,0:T(8,128)(2,1)}) custom-call(s32[8]{0:T(128)} %pad_add_fusion.4.eidx, s32[8]{0:T(128)} %stack.112.act, f32[4,8,256]{2,1,0:T(8,128)} %maximum_maximum_fusion.2.slots, ...), custom_call_target="tpu_custom_call" | custom-call | flops 34628173824 | bytes 90000000 | tf_op jit(solution)/shard_map/pallas_call | solution.py:218
  404.2 1.5 collective-permute-start.35
  405.7 84.1 %wgrad.1 = (f32[4,688,4096]{2,1,0:T(8,128)}, f32[4,688,4096]{2,1,0:T(8,128)}, f32[4,688,4096]{2,1,0:T(8,128)}) custom-call(s32[9]{0:T(128)} %pad_add_fusion.3.info, bf16[6,256,4096]{2,1,0:T(8,128)(2,1)} %get-tuple-element.70.xa.xoa, bf16[6,256,4096]{2,1,0:T(8,128)(2,1)} %get-tuple-element.85.xb.xob, bf16[6,256,4096]{2,1,0:T(8,128)(2,1)} %get-tuple-element.86.ga.goa, ...), custom_call_target="tpu_custom_call" | custom-call | flops 51942260736 | bytes 200000000 | tf_op jit(solution)/shard_map/wgrad/pallas_call | solution.py:372
  489.9 0.7 fusion.18
  490.6 0.7 add_bitcast_fusion
  491.3 0.8 copy-done.1
  492.1 6.1 %add_convert_fusion = bf16[256,4096]{1,0:T(8,128)(2,1)} fusion(f32[256,4096]{1,0:T(8,128)S(1)} %fusion.18, f32[256,4096]{1,0:T(8,128)} %collective-permute-done.36, f32[256,4096]{1,0:T(8,128)S(1)} %copy-done.1, f32[256,4096]{1,0:T(8,128)} %collective-permute-done.26), kind=kLoop, calls=%fused_computation.1 | loop fusion | flops 4194304 | bytes 18874368 | tf_op jit(solution)/shard_map/convert_element_type | solution.py:502
  (110 shorter events, 11.8 us)
Async XLA Ops:
  0.6 5.2 %copy-start = (bf16[4096,16]{0,1:T(8,128)(2,1)S(1)}, bf16[4096,16]{0,1:T(8,128)(2,1)}, u32[]{:S(2)}) copy-start(bf16[4096,16]{0,1:T(8,128)(2,1)} %param.9) | copy-start | bytes 393220
  0.6 7.4 %copy-start.2 = (s32[256,4]{0,1:T(4,128)S(1)}, s32[256,4]{0,1:T(4,128)}, u32[]{:S(2)}) copy-start(s32[256,4]{0,1:T(4,128)} %param.8) | copy-start | bytes 12292
  0.7 49.4 %collective-permute-start.4 = (bf16[256,4096]{1,0:T(8,128)(2,1)}, bf16[256,4096]{1,0:T(8,128)(2,1)}, u32[]{:S(2)}, u32[]{:S(2)}) collective-permute-start(bf16[256,4096]{1,0:T(8,128)(2,1)} %refs_0_.2), channel_id=1, source_target_pairs={{0,2},{1,3},{2,0},{3,1},{4,6},{5,7},{6,4},{7,5}} | collective-permute-start | bytes 6291464 | tf_op jit(solution)/shard_map/ppermute | solution.py:392
  4.0 46.2 %collective-permute-start.2 = (s32[4,256]{1,0:T(4,128)}, s32[4,256]{1,0:T(4,128)S(1)}, u32[]{:S(2)}, u32[]{:S(2)}) collective-permute-start(s32[4,256]{1,0:T(4,128)} %bitcast.89), channel_id=1, source_target_pairs={{0,3},{1,2},{2,1},{3,0},{4,7},{5,6},{6,5},{7,4}} | collective-permute-start | bytes 12296 | tf_op jit(solution)/shard_map/ppermute | solution.py:392
  4.0 48.9 %collective-permute-start.1 = (s32[4,256]{1,0:T(4,128)}, s32[4,256]{1,0:T(4,128)S(1)}, u32[]{:S(2)}, u32[]{:S(2)}) collective-permute-start(s32[4,256]{1,0:T(4,128)} %bitcast.90), channel_id=1, source_target_pairs={{0,2},{1,3},{2,0},{3,1},{4,6},{5,7},{6,4},{7,5}} | collective-permute-start | bytes 12296 | tf_op jit(solution)/shard_map/ppermute | solution.py:392
  5.2 48.1 %collective-permute-start = (s32[4,256]{1,0:T(4,128)}, s32[4,256]{1,0:T(4,128)S(1)}, u32[]{:S(2)}, u32[]{:S(2)}) collective-permute-start(s32[4,256]{1,0:T(4,128)} %bitcast.91), channel_id=1, source_target_pairs={{0,1},{1,0},{2,3},{3,2},{4,5},{5,4},{6,7},{7,6}} | collective-permute-start | bytes 12296 | tf_op jit(solution)/shard_map/ppermute | solution.py:392
  5.8 114.5 %collective-permute-start.3 = (bf16[256,4096]{1,0:T(8,128)(2,1)}, bf16[256,4096]{1,0:T(8,128)(2,1)}, u32[]{:S(2)}, u32[]{:S(2)}) collective-permute-start(bf16[256,4096]{1,0:T(8,128)(2,1)} %refs_0_.2), channel_id=1, source_target_pairs={{0,1},{1,0},{2,3},{3,2},{4,5},{5,4},{6,7},{7,6}} | collective-permute-start | bytes 6291464 | tf_op jit(solution)/shard_map/ppermute | solution.py:392
  50.0 71.8 %collective-permute-start.5 = (bf16[256,4096]{1,0:T(8,128)(2,1)}, bf16[256,4096]{1,0:T(8,128)(2,1)}, u32[]{:S(2)}, u32[]{:S(2)}) collective-permute-start(bf16[256,4096]{1,0:T(8,128)(2,1)} %collective-permute-done.4.refs_2_), channel_id=1, source_target_pairs={{0,1},{1,0},{2,3},{3,2},{4,5},{5,4},{6,7},{7,6}} | collective-permute-start | bytes 6291464 | tf_op jit(solution)/shard_map/ppermute | solution.py:392
  50.2 5.0 collective-permute-start.17
  52.9 4.1 collective-permute-start.16
  53.2 4.3 collective-permute-start.15
  55.2 4.0 collective-permute-start.18
  57.0 106.7 %collective-permute-start.7 = (bf16[256,4096]{1,0:T(8,128)(2,1)}, bf16[256,4096]{1,0:T(8,128)(2,1)}, u32[]{:S(2)}, u32[]{:S(2)}) collective-permute-start(bf16[256,4096]{1,0:T(8,128)(2,1)} %refs_0_.3), channel_id=1, source_target_pairs={{0,4},{1,5},{2,6},{3,7},{4,0},{5,1},{6,2},{7,3}} | collective-permute-start | bytes 6291464 | tf_op jit(solution)/shard_map/ppermute | solution.py:392
  57.5 106.2 %collective-permute-start.6 = (bf16[256,4096]{1,0:T(8,128)(2,1)}, bf16[256,4096]{1,0:T(8,128)(2,1)}, u32[]{:S(2)}, u32[]{:S(2)}) collective-permute-start(bf16[256,4096]{1,0:T(8,128)(2,1)} %refs_0_.3), channel_id=1, source_target_pairs={{0,2},{1,3},{2,0},{3,1},{4,6},{5,7},{6,4},{7,5}} | collective-permute-start | bytes 6291464 | tf_op jit(solution)/shard_map/ppermute | solution.py:392
  59.1 48.2 %collective-permute-start.14 = (f32[16,256]{1,0:T(8,128)S(1)}, f32[16,256]{1,0:T(8,128)S(1)}, u32[]{:S(2)}, u32[]{:S(2)}) collective-permute-start(f32[16,256]{1,0:T(8,128)S(1)} %bitcast.81), channel_id=1, source_target_pairs={{0,7},{1,6},{2,5},{3,4},{4,3},{5,2},{6,1},{7,0}} | collective-permute-start | bytes 49160 | tf_op jit(solution)/shard_map/ppermute | solution.py:392
  107.4 4.6 collective-permute-start.13
  112.0 3.2 collective-permute-start.12
  115.2 5.1 %collective-permute-start.11 = (f32[16,256]{1,0:T(8,128)S(1)}, f32[16,256]{1,0:T(8,128)S(1)}, u32[]{:S(2)}, u32[]{:S(2)}) collective-permute-start(f32[16,256]{1,0:T(8,128)S(1)} %bitcast.84), channel_id=1, source_target_pairs={{0,4},{1,5},{2,6},{3,7},{4,0},{5,1},{6,2},{7,3}} | collective-permute-start | bytes 49160 | tf_op jit(solution)/shard_map/ppermute | solution.py:392
  120.3 43.3 %collective-permute-start.10 = (f32[16,256]{1,0:T(8,128)S(1)}, f32[16,256]{1,0:T(8,128)S(1)}, u32[]{:S(2)}, u32[]{:S(2)}) collective-permute-start(f32[16,256]{1,0:T(8,128)S(1)} %bitcast.85), channel_id=1, source_target_pairs={{0,3},{1,2},{2,1},{3,0},{4,7},{5,6},{6,5},{7,4}} | collective-permute-start | bytes 49160 | tf_op jit(solution)/shard_map/ppermute | solution.py:392
  120.3 43.4 %collective-permute-start.9 = (f32[16,256]{1,0:T(8,128)S(1)}, f32[16,256]{1,0:T(8,128)S(1)}, u32[]{:S(2)}, u32[]{:S(2)}) collective-permute-start(f32[16,256]{1,0:T(8,128)S(1)} %bitcast.86), channel_id=1, source_target_pairs={{0,2},{1,3},{2,0},{3,1},{4,6},{5,7},{6,4},{7,5}} | collective-permute-start | bytes 49160 | tf_op jit(solution)/shard_map/ppermute | solution.py:392
  121.8 42.0 %collective-permute-start.8 = (f32[16,256]{1,0:T(8,128)S(1)}, f32[16,256]{1,0:T(8,128)S(1)}, u32[]{:S(2)}, u32[]{:S(2)}) collective-permute-start(f32[16,256]{1,0:T(8,128)S(1)} %bitcast.87), channel_id=1, source_target_pairs={{0,1},{1,0},{2,3},{3,2},{4,5},{5,4},{6,7},{7,6}} | collective-permute-start | bytes 49160 | tf_op jit(solution)/shard_map/ppermute | solution.py:392
  163.6 7.0 %collective-permute-start.19 = (bf16[256,4096]{1,0:T(8,128)(2,1)}, bf16[256,4096]{1,0:T(8,128)(2,1)}, u32[]{:S(2)}, u32[]{:S(2)}) collective-permute-start(bf16[256,4096]{1,0:T(8,128)(2,1)} %refs_0_.3), channel_id=1, source_target_pairs={{0,1},{1,0},{2,3},{3,2},{4,5},{5,4},{6,7},{7,6}} | collective-permute-start | bytes 6291464 | tf_op jit(solution)/shard_map/ppermute | solution.py:392
  163.8 7.4 %collective-permute-start.20 = (bf16[256,4096]{1,0:T(8,128)(2,1)}, bf16[256,4096]{1,0:T(8,128)(2,1)}, u32[]{:S(2)}, u32[]{:S(2)}) collective-permute-start(bf16[256,4096]{1,0:T(8,128)(2,1)} %collective-permute-done.6.refs_2_), channel_id=1, source_target_pairs={{0,1},{1,0},{2,3},{3,2},{4,5},{5,4},{6,7},{7,6}} | collective-permute-start | bytes 6291464 | tf_op jit(solution)/shard_map/ppermute | solution.py:392
  167.4 104.4 %collective-permute-start.21 = (bf16[256,4096]{1,0:T(8,128)(2,1)}, bf16[256,4096]{1,0:T(8,128)(2,1)}, u32[]{:S(2)}, u32[]{:S(2)}) collective-permute-start(bf16[256,4096]{1,0:T(8,128)(2,1)} %collective-permute-done.4.refs_2_), channel_id=1, source_target_pairs={{0,4},{1,5},{2,6},{3,7},{4,0},{5,1},{6,2},{7,3}} | collective-permute-start | bytes 6291464 | tf_op jit(solution)/shard_map/ppermute | solution.py:392
  168.9 104.5 %collective-permute-start.22 = (bf16[256,4096]{1,0:T(8,128)(2,1)}, bf16[256,4096]{1,0:T(8,128)(2,1)}, u32[]{:S(2)}, u32[]{:S(2)}) collective-permute-start(bf16[256,4096]{1,0:T(8,128)(2,1)} %collective-permute-done.6.refs_2_), channel_id=1, source_target_pairs={{0,4},{1,5},{2,6},{3,7},{4,0},{5,1},{6,2},{7,3}} | collective-permute-start | bytes 6291464 | tf_op jit(solution)/shard_map/ppermute | solution.py:392
  266.8 53.4 %collective-permute-start.31 = (f32[256,4096]{1,0:T(8,128)}, f32[256,4096]{1,0:T(8,128)}, u32[]{:S(2)}, u32[]{:S(2)}) collective-permute-start(f32[256,4096]{1,0:T(8,128)} %get-tuple-element.78), channel_id=1, source_target_pairs={{0,1},{1,0},{2,3},{3,2},{4,5},{5,4},{6,7},{7,6}} | collective-permute-start | bytes 12582920 | tf_op jit(solution)/shard_map/ppermute | solution.py:392
  267.1 48.1 %collective-permute-start.27 = (bf16[256,4096]{1,0:T(8,128)(2,1)}, bf16[256,4096]{1,0:T(8,128)(2,1)}, u32[]{:S(2)}, u32[]{:S(2)}) collective-permute-start(bf16[256,4096]{1,0:T(8,128)(2,1)} %refs_0_.2), channel_id=1, source_target_pairs={{0,4},{1,5},{2,6},{3,7},{4,0},{5,1},{6,2},{7,3}} | collective-permute-start | bytes 6291464 | tf_op jit(solution)/shard_map/ppermute | solution.py:392
  271.7 3.1 collective-permute-start.25
  271.8 3.6 collective-permute-start.24
  273.3 2.1 collective-permute-start.23
  275.4 50.8 %collective-permute-start.29 = (bf16[256,4096]{1,0:T(8,128)(2,1)}, bf16[256,4096]{1,0:T(8,128)(2,1)}, u32[]{:S(2)}, u32[]{:S(2)}) collective-permute-start(bf16[256,4096]{1,0:T(8,128)(2,1)} %collective-permute-done.21.refs_2_), channel_id=1, source_target_pairs={{0,1},{1,0},{2,3},{3,2},{4,5},{5,4},{6,7},{7,6}} | collective-permute-start | bytes 6291464 | tf_op jit(solution)/shard_map/ppermute | solution.py:392
  275.5 50.8 %collective-permute-start.30 = (bf16[256,4096]{1,0:T(8,128)(2,1)}, bf16[256,4096]{1,0:T(8,128)(2,1)}, u32[]{:S(2)}, u32[]{:S(2)}) collective-permute-start(bf16[256,4096]{1,0:T(8,128)(2,1)} %collective-permute-done.22.refs_6_), channel_id=1, source_target_pairs={{0,1},{1,0},{2,3},{3,2},{4,5},{5,4},{6,7},{7,6}} | collective-permute-start | bytes 6291464 | tf_op jit(solution)/shard_map/ppermute | solution.py:392
  315.2 18.6 %collective-permute-start.28 = (bf16[256,4096]{1,0:T(8,128)(2,1)}, bf16[256,4096]{1,0:T(8,128)(2,1)}, u32[]{:S(2)}, u32[]{:S(2)}) collective-permute-start(bf16[256,4096]{1,0:T(8,128)(2,1)} %collective-permute-done.27.refs_0_), channel_id=1, source_target_pairs={{0,1},{1,0},{2,3},{3,2},{4,5},{5,4},{6,7},{7,6}} | collective-permute-start | bytes 6291464 | tf_op jit(solution)/shard_map/ppermute | solution.py:392
  315.2 18.6 %collective-permute-start.32 = (bf16[256,4096]{1,0:T(8,128)(2,1)}, bf16[256,4096]{1,0:T(8,128)(2,1)}, u32[]{:S(2)}, u32[]{:S(2)}) collective-permute-start(bf16[256,4096]{1,0:T(8,128)(2,1)} %collective-permute-done.7.refs_4_), channel_id=1, source_target_pairs={{0,1},{1,0},{2,3},{3,2},{4,5},{5,4},{6,7},{7,6}} | collective-permute-start | bytes 6291464 | tf_op jit(solution)/shard_map/ppermute | solution.py:392
  326.3 5.8 %collective-permute-start.33 = (f32[16,4096]{1,0:T(8,128)S(1)}, f32[16,4096]{1,0:T(8,128)S(1)}, u32[]{:S(2)}, u32[]{:S(2)}) collective-permute-start(f32[16,4096]{1,0:T(8,128)S(1)} %fusion.17), channel_id=1, source_target_pairs={{0,1},{1,0},{2,3},{3,2},{4,5},{5,4},{6,7},{7,6}} | collective-permute-start | bytes 786440 | tf_op jit(solution)/shard_map/ppermute | solution.py:392
  331.2 160.1 %collective-permute-start.26 = (f32[256,4096]{1,0:T(8,128)}, f32[256,4096]{1,0:T(8,128)}, u32[]{:S(2)}, u32[]{:S(2)}) collective-permute-start(f32[256,4096]{1,0:T(8,128)} %get-tuple-element.68), channel_id=1, source_target_pairs={{0,1},{1,0},{2,3},{3,2},{4,5},{5,4},{6,7},{7,6}} | collective-permute-start | bytes 12582920 | tf_op jit(solution)/shard_map/ppermute | solution.py:392
  331.7 158.1 %collective-permute-start.36 = (f32[256,4096]{1,0:T(8,128)}, f32[256,4096]{1,0:T(8,128)}, u32[]{:S(2)}, u32[]{:S(2)}) collective-permute-start(f32[256,4096]{1,0:T(8,128)} %add.117), channel_id=1, source_target_pairs={{0,2},{1,3},{2,0},{3,1},{4,6},{5,7},{6,4},{7,5}} | collective-permute-start | bytes 12582920 | tf_op jit(solution)/shard_map/ppermute | solution.py:392
  332.1 72.0 %collective-permute-start.34 = (f32[16,4096]{1,0:T(8,128)S(1)}, f32[16,4096]{1,0:T(8,128)S(1)}, u32[]{:S(2)}, u32[]{:S(2)}) collective-permute-start(f32[16,4096]{1,0:T(8,128)S(1)} %add.119), channel_id=1, source_target_pairs={{0,4},{1,5},{2,6},{3,7},{4,0},{5,1},{6,2},{7,3}} | collective-permute-start | bytes 786440 | tf_op jit(solution)/shard_map/ppermute | solution.py:392
  404.2 85.6 %collective-permute-start.35 = (f32[16,4096]{1,0:T(8,128)S(1)}, f32[16,4096]{1,0:T(8,128)S(1)}, u32[]{:S(2)}, u32[]{:S(2)}) collective-permute-start(f32[16,4096]{1,0:T(8,128)S(1)} %add.120), channel_id=1, source_target_pairs={{0,2},{1,3},{2,0},{3,1},{4,6},{5,7},{6,4},{7,5}} | collective-permute-start | bytes 786440 | tf_op jit(solution)/shard_map/ppermute | solution.py:392
  489.8 2.3 copy-start.1

commit v2 on v1

--- a/solution.py
+++ b/solution.py
@@ -48,8 +48,9 @@
     acc = take(3 if mode == "both" else 2)
     zs = take(2 * (mode == "grad"))
     g_sc = take(1 * (mode == "grad"))
-    wbuf, wsem = take(2)
+    sel, wbuf, wsem = take(3)
     zsem = take(1 * (mode != "both"))
+    col = take(1 * has_g)
     c = pl.program_id(0)
 
     def w_copies(f, expert, slot):
@@ -79,18 +80,31 @@
         if mode == "grad":
             each_active(lambda i: [copy.start() for copy in z_copies(i)])
 
-    def gather(k, row, gate, base, n, tile, lo):
-        want = lax.broadcasted_iota(jnp.int32, (n, 256), 0) + base
-        hit = row == want.astype(F32)
-        sel = jnp.where(hit, 1.0, 0.0).astype(BF16)
+    @pl.when(c == 0)
+    def _():
+        for k in range(4):
+            for m in range(5):
+                n = OVER if m == 4 else COLD
+                lo = COLD * m
+                row = (lax.broadcasted_iota(jnp.int32, (n, 256), 0) + lo).astype(F32)
+                hit = slots[k, m:m + 1, :] == row
+                sel[k, lo:lo + n, :] = jnp.where(hit, 1.0, 0.0).astype(BF16)
+                if has_g:
+                    col[0][k, lo:lo + n, :] = jnp.sum(jnp.where(hit, gates[k, m:m + 1, :], 0.0), axis=1, keepdims=True)
+
+    def put(out, k, rows):
+        for j in range(4):
+            out[j, COLD * k:COLD * (k + 1), :] = rows[COLD * j:COLD * (j + 1)]
+        out[4 + k // 2, OVER * (k % 2):OVER * (k % 2) + OVER, :] = rows[256:384]
+
+    for k in range(4):
         if has_x:
-            x_out[0][tile, lo:lo + n, :] = mm(sel, xs[k][...], NN).astype(BF16)
+            put(x_out[0], k, mm(sel[k], xs[k][...], NN).astype(BF16))
         if has_g:
-            rows = mm(sel, gs[k][...], NN)
-            col = jnp.sum(jnp.where(hit, gate, 0.0), axis=1, keepdims=True)
-            do_out[0][tile, lo:lo + n, :] = (col * rows).astype(BF16)
+            rows = mm(sel[k], gs[k][...], NN)
+            put(do_out[0], k, (col[0][k] * rows).astype(BF16))
             if mode == "grad":
-                g_sc[0][lo:lo + n, :] = rows.astype(BF16)
+                put(g_sc[0], k, rows.astype(BF16))
 
     def finish(i, tile, lo):
         n = 128
@@ -127,17 +141,8 @@
                 for copy in ring_copies(f + ring - 1):
                     copy.start()
 
-            for k in range(4):
-                gather(k, slots[k, pl.ds(expert, 1), :], gates[k, pl.ds(expert, 1), :], expert * COLD, COLD, tile, COLD * k)
             for copy in ring_copies(f):
                 copy.wait()
-
-        for q in range(2):
-            @pl.when(i == 4 + 2 * q)
-            def _():
-                for half in range(2):
-                    k = 2 * q + half
-                    gather(k, slots[k, 4:5, :], gates[k, 4:5, :], 4 * COLD, OVER, 4 + q, OVER * half)
 
         @pl.when((act[i] == 1) & stray)
         def _():
@@ -158,7 +163,7 @@
             if has_g:
                 add(acc[0 if mode == "grad" else 2], mm(wbuf[slot, n_w - 1], do_out[0][tile], NT))
             if mode == "grad":
-                add(acc[1], mm(wbuf[slot, 0], g_sc[0][...], NT))
+                add(acc[1], mm(wbuf[slot, 0], g_sc[0][tile], NT))
 
         @pl.when((act[i] == 1) & (c == n_c - 1))
         def _():
@@ -209,10 +214,12 @@
     n_acc = 3 if mode == "both" else 2
     scratch = [pltpu.VMEM((8, ff, 256), F32)] * (n_acc + len(zs))
     if mode == "grad":
-        scratch.append(pltpu.VMEM((256, dc), BF16))
-    scratch += [pltpu.VMEM((ring + 1, len(weights), ff, dc), BF16), pltpu.SemaphoreType.DMA((ring + 1, len(weights)))]
+        scratch.append(pltpu.VMEM((6, 256, dc), BF16))
+    scratch += [pltpu.VMEM((4, 384, 256), BF16), pltpu.VMEM((ring + 1, len(weights), ff, dc), BF16), pltpu.SemaphoreType.DMA((ring + 1, len(weights)))]
     if mode != "both":
         scratch.append(pltpu.SemaphoreType.DMA((2, 8)))
+    if has_g:
+        scratch.append(pltpu.VMEM((4, 384, 1), F32))
     n_v = len(xs) + len(gs)
     n_mm = 4 if mode == "both" else 2
     return pl.pallas_call(
@@ -227,61 +234,95 @@
     )(eidx, act, slots, gates, *xs, *gs, *weights, *zs)
 
 
-def back_kernel(eidx, act, d1, d3, w1, w3, s0, s1, s2, s3, o0, o1, o2, o3, r_sc):
-    step = pl.program_id(1)
+def back_kernel(n_c, dc, ring, eidx, act, d1, d3, w1_hbm, w3_hbm, s0, s1, s2, s3, o0, o1, o2, o3, r_sc, sel, wbuf, wsem):
+    c = pl.program_id(0)
     slots, outs = (s0, s1, s2, s3), (o0, o1, o2, o3)
 
-    def rows(cols):
-        r = (mm(d1[0], w1[0, :, cols], NN) + mm(d3[0], w3[0, :, cols], NN)).astype(BF16)
-
-        @pl.when(step < 4)
-        def _():
-            lo = pl.multiple_of(eidx[step] * COLD, COLD)
-            for k in range(4):
-                r_sc[k, pl.ds(lo, COLD), cols] = r[COLD * k:COLD * (k + 1)]
-
-        for q in range(2):
-            @pl.when(step == 4 + 2 * q)
-            def _():
-                r_sc[2 * q, 256:384, cols] = r[0:128]
-
-            @pl.when((step == 4 + 2 * q) | (step == 5 + 2 * q))
-            def _():
-                r_sc[2 * q + 1, 256:384, cols] = r[128:256]
-
-    @pl.when(act[step] == 1)
+    def w_copies(f, expert, slot):
+        cols = pl.ds(pl.multiple_of((f // 4) * dc, dc), dc)
+        return [pltpu.make_async_copy(w.at[expert, :, cols], wbuf.at[slot, n], wsem.at[slot, n])
+                for n, w in enumerate((w1_hbm, w3_hbm))]
+
+    def ring_copies(f):
+        return w_copies(f, eidx[lax.rem(f, 4)], lax.rem(f, ring))
+
+    @pl.when(c == 0)
     def _():
-        def body(h, _):
-            rows(pl.ds(pl.multiple_of(h * 1024, 1024), 1024))
-            return 0
-
-        lax.fori_loop(0, w1.shape[2] // 1024, body, 0)
-
-    @pl.when(step == 7)
-    def _():
+        for f in range(ring - 1):
+            for copy in ring_copies(jnp.int32(f)):
+                copy.start()
         lane = lax.broadcasted_iota(jnp.int32, (256, 384), 1).astype(F32)
         for k in range(4):
             hit = lane == slots[k][:, 0:1]
             for m in range(1, 5):
                 hit = hit | (lane == slots[k][:, m:m + 1])
-            sel = jnp.where(hit, 1.0, 0.0).astype(BF16)
-            outs[k][...] = mm(sel, r_sc[k], NN)
+            sel[k] = jnp.where(hit, 1.0, 0.0).astype(BF16)
+
+    def step(i, _):
+        expert = eidx[i]
+        tile = tile_of(i, eidx)
+        f = c * 4 + jnp.minimum(i, 3)
+        stray = (i >= 4) & (expert != eidx[3])
+        slot = jnp.where(stray, ring, lax.rem(f, ring))
+
+        @pl.when(i < 4)
+        def _():
+            @pl.when(f + ring - 1 < 4 * n_c)
+            def _():
+                for copy in ring_copies(f + ring - 1):
+                    copy.start()
+
+            for copy in ring_copies(f):
+                copy.wait()
+
+        @pl.when((act[i] == 1) & stray)
+        def _():
+            for copy in w_copies(f, expert, ring):
+                copy.start()
+            for copy in w_copies(f, expert, ring):
+                copy.wait()
+
+        @pl.when(act[i] == 1)
+        def _():
+            r = (mm(d1[tile], wbuf[slot, 0], NN) + mm(d3[tile], wbuf[slot, 1], NN)).astype(BF16)
+
+            @pl.when(i < 4)
+            def _():
+                lo = pl.multiple_of(expert * COLD, COLD)
+                for k in range(4):
+                    r_sc[k, pl.ds(lo, COLD), :] = r[COLD * k:COLD * (k + 1)]
+
+            for q in range(2):
+                @pl.when(i == 4 + 2 * q)
+                def _():
+                    r_sc[2 * q, 256:384, :] = r[0:128]
+
+                @pl.when((i == 4 + 2 * q) | (i == 5 + 2 * q))
+                def _():
+                    r_sc[2 * q + 1, 256:384, :] = r[128:256]
+
+        return 0
+
+    lax.fori_loop(0, 8, step, 0)
+    for k in range(4):
+        outs[k][...] = mm(sel[k], r_sc[k], NN)
 
 
 def back(eidx, act, d1, d3, w1t, w3t, slots):
     ff, dim = w1t.shape[1:]
-    dc = 2048
-
-    d_blk = pl.BlockSpec((1, 256, ff), lambda c, i, e, t: (tile_of(i, e), 0, 0))
-    w_blk = pl.BlockSpec((1, ff, dc), lambda c, i, e, t: (e[i], 0, c))
-    s_blk = pl.BlockSpec((256, 8), lambda c, i, e, t: (0, 0))
-    o_blk = pl.BlockSpec((256, dc), lambda c, i, e, t: (0, c))
+    dc, ring = 1024, 4
+    n_c = dim // dc
+    d_blk = pl.BlockSpec((6, 256, ff), lambda c, e, t: (0, 0, 0), pipeline_mode=pl.Buffered(1))
+    any_blk = pl.BlockSpec(memory_space=pl.ANY)
+    s_blk = pl.BlockSpec((256, 8), lambda c, e, t: (0, 0))
     return pl.pallas_call(
-        back_kernel,
+        functools.partial(back_kernel, n_c, dc, ring),
         grid_spec=pltpu.PrefetchScalarGridSpec(
-            num_scalar_prefetch=2, grid=(dim // dc, 8),
-            in_specs=[d_blk, d_blk, w_blk, w_blk] + [s_blk] * 4, out_specs=[o_blk] * 4,
-            scratch_shapes=[pltpu.VMEM((4, 384, dc), BF16)]),
+            num_scalar_prefetch=2, grid=(n_c,),
+            in_specs=[d_blk, d_blk, any_blk, any_blk] + [s_blk] * 4,
+            out_specs=[pl.BlockSpec((256, dc), lambda c, e, t: (0, c))] * 4,
+            scratch_shapes=[pltpu.VMEM((4, 384, dc), BF16), pltpu.VMEM((4, 256, 384), BF16),
+                            pltpu.VMEM((ring + 1, 2, ff, dc), BF16), pltpu.SemaphoreType.DMA((ring + 1, 2))]),
         out_shape=[jax.ShapeDtypeStruct((256, dim), F32)] * 4,
         compiler_params=pltpu.CompilerParams(vmem_limit_bytes=VMEM_LIMIT),
         cost_estimate=cost(2 * 2 * 1536 * dim * ff, 70e6),
@@ -290,16 +331,16 @@
 
 
 def wgrad_kernel(info, xa, xb, ga, gb, xoa, xob, goa, gob,
-                 aa, d1a, d3a, ab, d1b, d3b, aoa, d1oa, d3oa, aob, d1ob, d3ob, w1o, w3o, w2o):
-    j = pl.program_id(0)
+                 aa, d1a, d3a, ab, d1b, d3b, w1o, w3o, w2o):
+    j = pl.program_id(1)
     all_hot = info[1] == j
     for m in range(2, 9):
         all_hot = all_hot & (info[m] == j)
 
     def run(first, second, cols):
         def part(n, q):
-            x, g, a, d1, d3 = n
-            return x[q, :, cols], g[q, :, cols], a[q], d1[q], d3[q]
+            (x, g, a, d1, d3), tile = n
+            return x[q, :, cols], g[q, :, cols], a[tile + q], d1[tile + q], d3[tile + q]
 
         def products(parts):
             w1o[0, :, cols] = sum(mm(p[3], p[0], NN) for p in parts)
@@ -337,8 +378,8 @@
 
                 lax.fori_loop(0, 2, body, 0)
 
-    na = ((xa, ga, aa, d1a, d3a), (xoa, goa, aoa, d1oa, d3oa), 1)
-    nb = ((xb, gb, ab, d1b, d3b), (xob, gob, aob, d1ob, d3ob), 5)
+    na = (((xa, ga, aa, d1a, d3a), j), ((xoa, goa, aa, d1a, d3a), 4), 1)
+    nb = (((xb, gb, ab, d1b, d3b), j), ((xob, gob, ab, d1b, d3b), 4), 5)
 
     def columns(h, _):
         cols = pl.ds(pl.multiple_of(h * 512, 512), 512)
@@ -359,27 +400,20 @@
 def wgrad(info, xa, ga, hid_a, xb, gb, hid_b, dim, ff):
     dc = 1024
 
-    def over(off):
-        def index(j, c, s):
-            used = (s[off] == j) | (s[off + 1] == j) | (s[off + 2] == j) | (s[off + 3] == j)
-            return 2, 0, jnp.where(used, c, 0)
-
-        return pl.BlockSpec((2, 256, dc), index)
-
-    main_blk = pl.BlockSpec((1, 256, dc), lambda j, c, s: (j, 0, c))
-    hid_blk = pl.BlockSpec((1, ff, 256), lambda j, c, s: (j, 0, 0))
-    hid_over = pl.BlockSpec((2, ff, 256), lambda j, c, s: (2, 0, 0))
+    main_blk = pl.BlockSpec((1, 256, dc), lambda c, j, s: (j, 0, c))
+    over_blk = pl.BlockSpec((2, 256, dc), lambda c, j, s: (2, 0, c))
+    hid_blk = pl.BlockSpec((6, ff, 256), lambda c, j, s: (0, 0, 0), pipeline_mode=pl.Buffered(1))
     return pl.pallas_call(
         wgrad_kernel,
         grid_spec=pltpu.PrefetchScalarGridSpec(
-            num_scalar_prefetch=1, grid=(4, dim // dc),
-            in_specs=[main_blk] * 4 + [over(1), over(5)] * 2 + [hid_blk] * 6 + [hid_over] * 6,
-            out_specs=[pl.BlockSpec((1, ff, dc), lambda j, c, s: (j, 0, c))] * 3),
+            num_scalar_prefetch=1, grid=(dim // dc, 4),
+            in_specs=[main_blk] * 4 + [over_blk] * 4 + [hid_blk] * 6,
+            out_specs=[pl.BlockSpec((1, ff, dc), lambda c, j, s: (j, 0, c))] * 3),
         out_shape=[jax.ShapeDtypeStruct((4, ff, dim), F32)] * 3,
         compiler_params=pltpu.CompilerParams(vmem_limit_bytes=VMEM_LIMIT),
         cost_estimate=cost(3 * 2 * 3072 * dim * ff, 200e6),
         name="wgrad",
-    )(info, xa, xb, ga, gb, xa, xb, ga, gb, *hid_a, *hid_b, *hid_a, *hid_b)
+    )(info, xa, xb, ga, gb, xa, xb, ga, gb, *hid_a, *hid_b)
 
 
 def solution(mesh):
@@ -449,7 +483,7 @@
         x_ys = shift(x_y, 0, 1)
         gate_a0 = jnp.zeros((4, 8, tok), F32)
         xa, z1_a, z3_a = experts("fwd", eidx_a, act_a, slots_a, gate_a0, (x_loc, x_sib, x_across, x_across_sib), (),
-                                 (w1t, w3t), (), 1024, 4)
+                                 (w1t, w3t), (), 2048, 3)
         z1_a, g_across, g_y, gates_a, gates_b, idx_b = lax.optimization_barrier((z1_a, g_across, g_y, gates_a, gates_b, idx_b))
         ranks_b, slots_b, hot_b, eidx_b, act_b = tables(idx_b)
         g_across_sib = shift(g_across, 0, 1)

time: 499 us -> 465 us (0.932)
  Pallas kernels: 291 us -> 252 us
  waiting for transfers between devices: 137 us -> 143 us
    pallas_call x3, Pallas kernels: 160 us -> 133 us  [experts(): pl.pallas_call(functools.partial(expert_kernel, mode, n_c, dc, ring), gri...]
    pallas_call x1, Pallas kernels: 46.7 us -> 37.8 us  [back(): pl.pallas_call(functools.partial(back_kernel, n_c, dc, ring), grid_spec=p...]
    ppermute x37, waiting for transfers between devices: 137 us -> 143 us  [shift(): return lax.ppermute(arr, axes, pairs)]
  transfers between devices with their start and end apart: 37 -> 37, of which waited for: 9 -> 9; matrix products, arithmetic and copies ran while one was open for 6% -> 6% of each run, Pallas kernels for 58% -> 54%
where the time goes in v2:
time: 465 us
  Pallas kernels  252 us (54%)
  waiting for transfers between devices  143 us (31%)
  starting transfers between devices  27.8 us (6%)
  other arithmetic  21.6 us (5%)
  local copies, waits for them, and re-layouts  9.48 us (2%)
  between operations  6.08 us (1%)
  matrix products  5.28 us (1%)
    ppermute x37, waiting for transfers between devices, shift(): return lax.ppermute(arr, axes, pairs)  143 us
    pallas_call x3, Pallas kernels, experts(): pl.pallas_call(functools.partial(expert_kernel, mode, n_c, dc, ring), gri...  133 us
    pallas_call x1, Pallas kernels, wgrad(): pl.pallas_call(wgrad_kernel, grid_spec=pltpu.PrefetchScalarGridSpec(num_s...  81.1 us
    pallas_call x1, Pallas kernels, back(): pl.pallas_call(functools.partial(back_kernel, n_c, dc, ring), grid_spec=p...  37.8 us
    ppermute x37, starting transfers between devices, shift(): return lax.ppermute(arr, axes, pairs)  27.8 us
  transfers between devices with their start and end apart: 37, of which 9 were waited for; matrix products, arithmetic and copies ran while one was open for 6% of the time, Pallas kernels for 54%

profile of v2, /device:TPU:0, one launch (start us, length us, event | category | flops | bytes accessed | tf_op | source)
XLA Modules:
  0.0 464.8 jit_solution(563249175283633824)
XLA Ops:
  0.7 3.3 collective-permute-start.4
  4.0 1.2 collective-permute-start.1
  5.2 0.7 collective-permute-start
  5.9 2.2 fusion.16
  8.2 41.9 %collective-permute-done.4.refs_2_ = bf16[256,4096]{1,0:T(8,128)(2,1)} collective-permute-done((bf16[256,4096]{1,0:T(8,128)(2,1)}, bf16[256,4096]{1,0:T(8,128)(2,1)}, u32[]{:S(2)}, u32[]{:S(2)}) %collective-permute-start.4) | collective-permute-done | bytes 2097184 | tf_op jit(solution)/shard_map/ppermute | solution.py:426
  50.2 2.7 collective-permute-start.17
  53.2 1.5 collective-permute-start.15
  55.2 1.2 collective-permute-start.18
  56.4 0.7 fusion.12
  57.5 1.4 collective-permute-start.6
  59.1 1.6 collective-permute-start.14
  60.8 46.5 %collective-permute-done.14 = f32[16,256]{1,0:T(8,128)S(1)} collective-permute-done((f32[16,256]{1,0:T(8,128)S(1)}, f32[16,256]{1,0:T(8,128)S(1)}, u32[]{:S(2)}, u32[]{:S(2)}) %collective-permute-start.14) | collective-permute-done | bytes 16416 | tf_op jit(solution)/shard_map/ppermute | solution.py:426
  108.0 4.0 collective-permute-done.13
  112.0 0.6 fusion.9
  112.7 2.5 collective-permute-done.12
  115.8 1.2 pad_add_fusion.2.eidx
  119.6 0.7 stack.99.act
  120.3 1.5 collective-permute-start.9
  122.8 33.0 %shard_map.110 = (bf16[6,256,4096]{2,1,0:T(8,128)(2,1)}, f32[8,688,256]{2,1,0:T(8,128)}, f32[8,688,256]{2,1,0:T(8,128)}) custom-call(s32[8]{0:T(128)} %pad_add_fusion.2.eidx, s32[8]{0:T(128)} %stack.99.act, f32[4,8,256]{2,1,0:T(8,128)} %get-tuple-element.115.slots, f32[4,8,256]{2,1,0:T(8,128)} %broadcast_in_dim.122.gates, bf16[256,4096]{1,0:T(8,128)(2,1)} %refs_0_.2, ...), custom_call_target="tpu_custom_call" | custom-call | flops 17314086912 | bytes 90000000 | tf_op jit(solution)/shard_map/pallas_call | solution.py:225
  156.5 0.8 copy.22.s3
  157.3 0.8 copy.21.s2
  158.0 0.8 copy.20.s1
  158.8 0.8 copy.19.s0
  159.6 1.4 collective-permute-start.21
  162.1 0.7 maximum_maximum_fusion.1
  163.3 42.1 %shard_map.111 = (bf16[6,256,4096]{2,1,0:T(8,128)(2,1)}, bf16[6,688,256]{2,1,0:T(8,128)(2,1)}, bf16[6,688,256]{2,1,0:T(8,128)(2,1)}, bf16[6,688,256]{2,1,0:T(8,1...) custom-call(s32[8]{0:T(128)} %pad_add_fusion.2.eidx, s32[8]{0:T(128)} %stack.99.act, ...), custom_call_target="tpu_custom_call" | custom-call | flops 17314086912 | bytes 90000000 | tf_op jit(solution)/shard_map/pallas_call | solution.py:225
  205.4 37.8 %back.1 = (f32[256,4096]{1,0:T(8,128)}, f32[256,4096]{1,0:T(8,128)}, f32[256,4096]{1,0:T(8,128)}, f32[256,4096]{1,0:T(8,128)}) custom-call(s32[8]{0:T(128)} %pad_add_fusion.2.eidx, s32[8]{0:T(128)} %stack.99.act, bf16[6,256,688]{2,1,0:T(8,128)(2,1)} %get-tuple-element.63.d1, bf16[6,256,688]{2,1,0:T(8,128)(2,1)} %get-tuple-element.64.d3, ...), custom_call_target="tpu_custom_call" | custom-call | flops 17314086912 | bytes 70000000 | tf_op jit(solution)/shard_map/back/pallas_call | solution.py:318
  243.3 1.4 collective-permute-start.27
  244.8 0.7 slice.72
  245.5 0.8 slice_reduce_fusion
  246.6 1.3 select_reduce_fusion
  248.2 1.5 collective-permute-start.24
  249.7 3.7 collective-permute-done.22.refs_6_
  253.4 1.2 collective-permute-done.23
  255.0 42.4 %collective-permute-done.27.refs_0_ = bf16[256,4096]{1,0:T(8,128)(2,1)} collective-permute-done((bf16[256,4096]{1,0:T(8,128)(2,1)}, bf16[256,4096]{1,0:T(8,128)(2,1)}, u32[]{:S(2)}, u32[]{:S(2)}) %collective-permute-start.27) | collective-permute-done | bytes 2097184 | tf_op jit(solution)/shard_map/ppermute | solution.py:426
  298.7 0.7 fusion.14
  300.5 2.0 fusion.17
  302.5 6.0 %add.117 = f32[256,4096]{1,0:T(8,128)} add(f32[256,4096]{1,0:T(8,128)} %get-tuple-element.77, f32[256,4096]{1,0:T(8,128)} %collective-permute-done.31) | non-fusion elementwise | flops 1048576 | bytes 12582912 | tf_op jit(solution)/shard_map/add | solution.py:513
  308.6 1.1 pad_add_fusion.4.eidx
  312.8 0.7 maximum_maximum_fusion.2.slots
  314.6 1.4 collective-permute-start.34
  316.1 57.7 %shard_map.112 = (bf16[6,256,4096]{2,1,0:T(8,128)(2,1)}, bf16[6,256,4096]{2,1,0:T(8,128)(2,1)}, bf16[6,688,256]{2,1,0:T(8,128)(2,1)}, bf16[6,688,256]{2,1,0:T(8,128)(2,1)}, bf16[6,688,256]{2,1,0:T(8,128)(2,1)}) custom-call(s32[8]{0:T(128)} %pad_add_fusion.4.eidx, s32[8]{0:T(128)} %stack.112.act, f32[4,8,256]{2,1,0:T(8,128)} %maximum_maximum_fusion.2.slots, ...), custom_call_target="tpu_custom_call" | custom-call | flops 34628173824 | bytes 90000000 | tf_op jit(solution)/shard_map/pallas_call | solution.py:225
  373.9 1.4 collective-permute-start.35
  375.3 81.1 %wgrad.1 = (f32[4,688,4096]{2,1,0:T(8,128)}, f32[4,688,4096]{2,1,0:T(8,128)}, f32[4,688,4096]{2,1,0:T(8,128)}) custom-call(s32[9]{0:T(128)} %pad_add_fusion.3.info, bf16[6,256,4096]{2,1,0:T(8,128)(2,1)} %get-tuple-element.70.xa.xoa, bf16[6,256,4096]{2,1,0:T(8,128)(2,1)} %get-tuple-element.85.xb.xob, bf16[6,256,4096]{2,1,0:T(8,128)(2,1)} %get-tuple-element.86.ga.goa, ...), custom_call_target="tpu_custom_call" | custom-call | flops 51942260736 | bytes 200000000 | tf_op jit(solution)/shard_map/wgrad/pallas_call | solution.py:406
  456.4 0.7 fusion.18
  457.1 0.7 add_bitcast_fusion
  457.9 0.8 copy-done.1
  458.7 6.1 %add_convert_fusion = bf16[256,4096]{1,0:T(8,128)(2,1)} fusion(f32[256,4096]{1,0:T(8,128)S(1)} %fusion.18, f32[256,4096]{1,0:T(8,128)} %collective-permute-done.36, f32[256,4096]{1,0:T(8,128)S(1)} %copy-done.1, f32[256,4096]{1,0:T(8,128)} %collective-permute-done.26), kind=kLoop, calls=%fused_computation.1 | loop fusion | flops 4194304 | bytes 18874368 | tf_op jit(solution)/shard_map/convert_element_type | solution.py:536
  (110 shorter events, 11.8 us)
Async XLA Ops:
  0.6 5.2 %copy-start = (bf16[4096,16]{0,1:T(8,128)(2,1)S(1)}, bf16[4096,16]{0,1:T(8,128)(2,1)}, u32[]{:S(2)}) copy-start(bf16[4096,16]{0,1:T(8,128)(2,1)} %param.9) | copy-start | bytes 393220
  0.6 7.4 %copy-start.2 = (s32[256,4]{0,1:T(4,128)S(1)}, s32[256,4]{0,1:T(4,128)}, u32[]{:S(2)}) copy-start(s32[256,4]{0,1:T(4,128)} %param.8) | copy-start | bytes 12292
  0.7 49.4 %collective-permute-start.4 = (bf16[256,4096]{1,0:T(8,128)(2,1)}, bf16[256,4096]{1,0:T(8,128)(2,1)}, u32[]{:S(2)}, u32[]{:S(2)}) collective-permute-start(bf16[256,4096]{1,0:T(8,128)(2,1)} %refs_0_.2), channel_id=1, source_target_pairs={{0,2},{1,3},{2,0},{3,1},{4,6},{5,7},{6,4},{7,5}} | collective-permute-start | bytes 6291464 | tf_op jit(solution)/shard_map/ppermute | solution.py:426
  4.0 46.2 %collective-permute-start.2 = (s32[4,256]{1,0:T(4,128)}, s32[4,256]{1,0:T(4,128)S(1)}, u32[]{:S(2)}, u32[]{:S(2)}) collective-permute-start(s32[4,256]{1,0:T(4,128)} %bitcast.89), channel_id=1, source_target_pairs={{0,3},{1,2},{2,1},{3,0},{4,7},{5,6},{6,5},{7,4}} | collective-permute-start | bytes 12296 | tf_op jit(solution)/shard_map/ppermute | solution.py:426
  4.0 48.9 %collective-permute-start.1 = (s32[4,256]{1,0:T(4,128)}, s32[4,256]{1,0:T(4,128)S(1)}, u32[]{:S(2)}, u32[]{:S(2)}) collective-permute-start(s32[4,256]{1,0:T(4,128)} %bitcast.90), channel_id=1, source_target_pairs={{0,2},{1,3},{2,0},{3,1},{4,6},{5,7},{6,4},{7,5}} | collective-permute-start | bytes 12296 | tf_op jit(solution)/shard_map/ppermute | solution.py:426
  5.2 48.1 %collective-permute-start = (s32[4,256]{1,0:T(4,128)}, s32[4,256]{1,0:T(4,128)S(1)}, u32[]{:S(2)}, u32[]{:S(2)}) collective-permute-start(s32[4,256]{1,0:T(4,128)} %bitcast.91), channel_id=1, source_target_pairs={{0,1},{1,0},{2,3},{3,2},{4,5},{5,4},{6,7},{7,6}} | collective-permute-start | bytes 12296 | tf_op jit(solution)/shard_map/ppermute | solution.py:426
  5.8 114.5 %collective-permute-start.3 = (bf16[256,4096]{1,0:T(8,128)(2,1)}, bf16[256,4096]{1,0:T(8,128)(2,1)}, u32[]{:S(2)}, u32[]{:S(2)}) collective-permute-start(bf16[256,4096]{1,0:T(8,128)(2,1)} %refs_0_.2), channel_id=1, source_target_pairs={{0,1},{1,0},{2,3},{3,2},{4,5},{5,4},{6,7},{7,6}} | collective-permute-start | bytes 6291464 | tf_op jit(solution)/shard_map/ppermute | solution.py:426
  50.0 71.8 %collective-permute-start.5 = (bf16[256,4096]{1,0:T(8,128)(2,1)}, bf16[256,4096]{1,0:T(8,128)(2,1)}, u32[]{:S(2)}, u32[]{:S(2)}) collective-permute-start(bf16[256,4096]{1,0:T(8,128)(2,1)} %collective-permute-done.4.refs_2_), channel_id=1, source_target_pairs={{0,1},{1,0},{2,3},{3,2},{4,5},{5,4},{6,7},{7,6}} | collective-permute-start | bytes 6291464 | tf_op jit(solution)/shard_map/ppermute | solution.py:426
  50.2 5.0 %collective-permute-start.17 = (s32[4,256]{1,0:T(4,128)S(1)}, s32[4,256]{1,0:T(4,128)S(1)}, u32[]{:S(2)}, u32[]{:S(2)}) collective-permute-start(s32[4,256]{1,0:T(4,128)S(1)} %bitcast.92), channel_id=1, source_target_pairs={{0,6},{1,7},{2,4},{3,5},{4,2},{5,3},{6,0},{7,1}} | collective-permute-start | bytes 12296 | tf_op jit(solution)/shard_map/ppermute | solution.py:426
  52.9 4.1 collective-permute-start.16
  53.2 4.3 collective-permute-start.15
  55.2 4.0 collective-permute-start.18
  57.0 98.9 %collective-permute-start.7 = (bf16[256,4096]{1,0:T(8,128)(2,1)}, bf16[256,4096]{1,0:T(8,128)(2,1)}, u32[]{:S(2)}, u32[]{:S(2)}) collective-permute-start(bf16[256,4096]{1,0:T(8,128)(2,1)} %refs_0_.3), channel_id=1, source_target_pairs={{0,4},{1,5},{2,6},{3,7},{4,0},{5,1},{6,2},{7,3}} | collective-permute-start | bytes 6291464 | tf_op jit(solution)/shard_map/ppermute | solution.py:426
  57.5 98.4 %collective-permute-start.6 = (bf16[256,4096]{1,0:T(8,128)(2,1)}, bf16[256,4096]{1,0:T(8,128)(2,1)}, u32[]{:S(2)}, u32[]{:S(2)}) collective-permute-start(bf16[256,4096]{1,0:T(8,128)(2,1)} %refs_0_.3), channel_id=1, source_target_pairs={{0,2},{1,3},{2,0},{3,1},{4,6},{5,7},{6,4},{7,5}} | collective-permute-start | bytes 6291464 | tf_op jit(solution)/shard_map/ppermute | solution.py:426
  59.1 48.2 %collective-permute-start.14 = (f32[16,256]{1,0:T(8,128)S(1)}, f32[16,256]{1,0:T(8,128)S(1)}, u32[]{:S(2)}, u32[]{:S(2)}) collective-permute-start(f32[16,256]{1,0:T(8,128)S(1)} %bitcast.81), channel_id=1, source_target_pairs={{0,7},{1,6},{2,5},{3,4},{4,3},{5,2},{6,1},{7,0}} | collective-permute-start | bytes 49160 | tf_op jit(solution)/shard_map/ppermute | solution.py:426
  107.4 4.6 collective-permute-start.13
  112.0 3.2 collective-permute-start.12
  115.2 5.1 %collective-permute-start.11 = (f32[16,256]{1,0:T(8,128)S(1)}, f32[16,256]{1,0:T(8,128)S(1)}, u32[]{:S(2)}, u32[]{:S(2)}) collective-permute-start(f32[16,256]{1,0:T(8,128)S(1)} %bitcast.84), channel_id=1, source_target_pairs={{0,4},{1,5},{2,6},{3,7},{4,0},{5,1},{6,2},{7,3}} | collective-permute-start | bytes 49160 | tf_op jit(solution)/shard_map/ppermute | solution.py:426
  120.3 35.5 %collective-permute-start.10 = (f32[16,256]{1,0:T(8,128)S(1)}, f32[16,256]{1,0:T(8,128)S(1)}, u32[]{:S(2)}, u32[]{:S(2)}) collective-permute-start(f32[16,256]{1,0:T(8,128)S(1)} %bitcast.85), channel_id=1, source_target_pairs={{0,3},{1,2},{2,1},{3,0},{4,7},{5,6},{6,5},{7,4}} | collective-permute-start | bytes 49160 | tf_op jit(solution)/shard_map/ppermute | solution.py:426
  120.3 35.6 %collective-permute-start.9 = (f32[16,256]{1,0:T(8,128)S(1)}, f32[16,256]{1,0:T(8,128)S(1)}, u32[]{:S(2)}, u32[]{:S(2)}) collective-permute-start(f32[16,256]{1,0:T(8,128)S(1)} %bitcast.86), channel_id=1, source_target_pairs={{0,2},{1,3},{2,0},{3,1},{4,6},{5,7},{6,4},{7,5}} | collective-permute-start | bytes 49160 | tf_op jit(solution)/shard_map/ppermute | solution.py:426
  121.8 34.2 %collective-permute-start.8 = (f32[16,256]{1,0:T(8,128)S(1)}, f32[16,256]{1,0:T(8,128)S(1)}, u32[]{:S(2)}, u32[]{:S(2)}) collective-permute-start(f32[16,256]{1,0:T(8,128)S(1)} %bitcast.87), channel_id=1, source_target_pairs={{0,1},{1,0},{2,3},{3,2},{4,5},{5,4},{6,7},{7,6}} | collective-permute-start | bytes 49160 | tf_op jit(solution)/shard_map/ppermute | solution.py:426
  155.8 7.0 %collective-permute-start.19 = (bf16[256,4096]{1,0:T(8,128)(2,1)}, bf16[256,4096]{1,0:T(8,128)(2,1)}, u32[]{:S(2)}, u32[]{:S(2)}) collective-permute-start(bf16[256,4096]{1,0:T(8,128)(2,1)} %refs_0_.3), channel_id=1, source_target_pairs={{0,1},{1,0},{2,3},{3,2},{4,5},{5,4},{6,7},{7,6}} | collective-permute-start | bytes 6291464 | tf_op jit(solution)/shard_map/ppermute | solution.py:426
  156.0 7.4 %collective-permute-start.20 = (bf16[256,4096]{1,0:T(8,128)(2,1)}, bf16[256,4096]{1,0:T(8,128)(2,1)}, u32[]{:S(2)}, u32[]{:S(2)}) collective-permute-start(bf16[256,4096]{1,0:T(8,128)(2,1)} %collective-permute-done.6.refs_2_), channel_id=1, source_target_pairs={{0,1},{1,0},{2,3},{3,2},{4,5},{5,4},{6,7},{7,6}} | collective-permute-start | bytes 6291464 | tf_op jit(solution)/shard_map/ppermute | solution.py:426
  159.6 88.6 %collective-permute-start.21 = (bf16[256,4096]{1,0:T(8,128)(2,1)}, bf16[256,4096]{1,0:T(8,128)(2,1)}, u32[]{:S(2)}, u32[]{:S(2)}) collective-permute-start(bf16[256,4096]{1,0:T(8,128)(2,1)} %collective-permute-done.4.refs_2_), channel_id=1, source_target_pairs={{0,4},{1,5},{2,6},{3,7},{4,0},{5,1},{6,2},{7,3}} | collective-permute-start | bytes 6291464 | tf_op jit(solution)/shard_map/ppermute | solution.py:426
  161.0 92.3 %collective-permute-start.22 = (bf16[256,4096]{1,0:T(8,128)(2,1)}, bf16[256,4096]{1,0:T(8,128)(2,1)}, u32[]{:S(2)}, u32[]{:S(2)}) collective-permute-start(bf16[256,4096]{1,0:T(8,128)(2,1)} %collective-permute-done.6.refs_2_), channel_id=1, source_target_pairs={{0,4},{1,5},{2,6},{3,7},{4,0},{5,1},{6,2},{7,3}} | collective-permute-start | bytes 6291464 | tf_op jit(solution)/shard_map/ppermute | solution.py:426
  243.2 59.3 %collective-permute-start.31 = (f32[256,4096]{1,0:T(8,128)}, f32[256,4096]{1,0:T(8,128)}, u32[]{:S(2)}, u32[]{:S(2)}) collective-permute-start(f32[256,4096]{1,0:T(8,128)} %get-tuple-element.78), channel_id=1, source_target_pairs={{0,1},{1,0},{2,3},{3,2},{4,5},{5,4},{6,7},{7,6}} | collective-permute-start | bytes 12582920 | tf_op jit(solution)/shard_map/ppermute | solution.py:426
  243.3 54.1 %collective-permute-start.27 = (bf16[256,4096]{1,0:T(8,128)(2,1)}, bf16[256,4096]{1,0:T(8,128)(2,1)}, u32[]{:S(2)}, u32[]{:S(2)}) collective-permute-start(bf16[256,4096]{1,0:T(8,128)(2,1)} %refs_0_.2), channel_id=1, source_target_pairs={{0,4},{1,5},{2,6},{3,7},{4,0},{5,1},{6,2},{7,3}} | collective-permute-start | bytes 6291464 | tf_op jit(solution)/shard_map/ppermute | solution.py:426
  247.9 5.4 %collective-permute-start.25 = (f32[4,256]{1,0:T(4,128)S(1)}, f32[4,256]{1,0:T(4,128)S(1)}, u32[]{:S(2)}, u32[]{:S(2)}) collective-permute-start(f32[4,256]{1,0:T(4,128)S(1)} %get-tuple-element.117), channel_id=1, source_target_pairs={{0,3},{1,2},{2,1},{3,0},{4,7},{5,6},{6,5},{7,4}} | collective-permute-start | bytes 12296 | tf_op jit(solution)/shard_map/ppermute | solution.py:426
  248.2 5.1 %collective-permute-start.24 = (f32[4,256]{1,0:T(4,128)S(1)}, f32[4,256]{1,0:T(4,128)S(1)}, u32[]{:S(2)}, u32[]{:S(2)}) collective-permute-start(f32[4,256]{1,0:T(4,128)S(1)} %get-tuple-element.118), channel_id=1, source_target_pairs={{0,2},{1,3},{2,0},{3,1},{4,6},{5,7},{6,4},{7,5}} | collective-permute-start | bytes 12296 | tf_op jit(solution)/shard_map/ppermute | solution.py:426
  253.4 1.2 collective-permute-start.23
  254.5 54.0 %collective-permute-start.29 = (bf16[256,4096]{1,0:T(8,128)(2,1)}, bf16[256,4096]{1,0:T(8,128)(2,1)}, u32[]{:S(2)}, u32[]{:S(2)}) collective-permute-start(bf16[256,4096]{1,0:T(8,128)(2,1)} %collective-permute-done.21.refs_2_), channel_id=1, source_target_pairs={{0,1},{1,0},{2,3},{3,2},{4,5},{5,4},{6,7},{7,6}} | collective-permute-start | bytes 6291464 | tf_op jit(solution)/shard_map/ppermute | solution.py:426
  254.7 53.9 %collective-permute-start.30 = (bf16[256,4096]{1,0:T(8,128)(2,1)}, bf16[256,4096]{1,0:T(8,128)(2,1)}, u32[]{:S(2)}, u32[]{:S(2)}) collective-permute-start(bf16[256,4096]{1,0:T(8,128)(2,1)} %collective-permute-done.22.refs_6_), channel_id=1, source_target_pairs={{0,1},{1,0},{2,3},{3,2},{4,5},{5,4},{6,7},{7,6}} | collective-permute-start | bytes 6291464 | tf_op jit(solution)/shard_map/ppermute | solution.py:426
  297.4 18.6 %collective-permute-start.28 = (bf16[256,4096]{1,0:T(8,128)(2,1)}, bf16[256,4096]{1,0:T(8,128)(2,1)}, u32[]{:S(2)}, u32[]{:S(2)}) collective-permute-start(bf16[256,4096]{1,0:T(8,128)(2,1)} %collective-permute-done.27.refs_0_), channel_id=1, source_target_pairs={{0,1},{1,0},{2,3},{3,2},{4,5},{5,4},{6,7},{7,6}} | collective-permute-start | bytes 6291464 | tf_op jit(solution)/shard_map/ppermute | solution.py:426
  297.5 18.6 %collective-permute-start.32 = (bf16[256,4096]{1,0:T(8,128)(2,1)}, bf16[256,4096]{1,0:T(8,128)(2,1)}, u32[]{:S(2)}, u32[]{:S(2)}) collective-permute-start(bf16[256,4096]{1,0:T(8,128)(2,1)} %collective-permute-done.7.refs_4_), channel_id=1, source_target_pairs={{0,1},{1,0},{2,3},{3,2},{4,5},{5,4},{6,7},{7,6}} | collective-permute-start | bytes 6291464 | tf_op jit(solution)/shard_map/ppermute | solution.py:426
  308.6 6.0 %collective-permute-start.33 = (f32[16,4096]{1,0:T(8,128)S(1)}, f32[16,4096]{1,0:T(8,128)S(1)}, u32[]{:S(2)}, u32[]{:S(2)}) collective-permute-start(f32[16,4096]{1,0:T(8,128)S(1)} %fusion.17), channel_id=1, source_target_pairs={{0,1},{1,0},{2,3},{3,2},{4,5},{5,4},{6,7},{7,6}} | collective-permute-start | bytes 786440 | tf_op jit(solution)/shard_map/ppermute | solution.py:426
  313.5 144.4 %collective-permute-start.26 = (f32[256,4096]{1,0:T(8,128)}, f32[256,4096]{1,0:T(8,128)}, u32[]{:S(2)}, u32[]{:S(2)}) collective-permute-start(f32[256,4096]{1,0:T(8,128)} %get-tuple-element.68), channel_id=1, source_target_pairs={{0,1},{1,0},{2,3},{3,2},{4,5},{5,4},{6,7},{7,6}} | collective-permute-start | bytes 12582920 | tf_op jit(solution)/shard_map/ppermute | solution.py:426
  314.0 142.4 %collective-permute-start.36 = (f32[256,4096]{1,0:T(8,128)}, f32[256,4096]{1,0:T(8,128)}, u32[]{:S(2)}, u32[]{:S(2)}) collective-permute-start(f32[256,4096]{1,0:T(8,128)} %add.117), channel_id=1, source_target_pairs={{0,2},{1,3},{2,0},{3,1},{4,6},{5,7},{6,4},{7,5}} | collective-permute-start | bytes 12582920 | tf_op jit(solution)/shard_map/ppermute | solution.py:426
  314.6 59.2 %collective-permute-start.34 = (f32[16,4096]{1,0:T(8,128)S(1)}, f32[16,4096]{1,0:T(8,128)S(1)}, u32[]{:S(2)}, u32[]{:S(2)}) collective-permute-start(f32[16,4096]{1,0:T(8,128)S(1)} %add.119), channel_id=1, source_target_pairs={{0,4},{1,5},{2,6},{3,7},{4,0},{5,1},{6,2},{7,3}} | collective-permute-start | bytes 786440 | tf_op jit(solution)/shard_map/ppermute | solution.py:426
  373.9 82.5 %collective-permute-start.35 = (f32[16,4096]{1,0:T(8,128)S(1)}, f32[16,4096]{1,0:T(8,128)S(1)}, u32[]{:S(2)}, u32[]{:S(2)}) collective-permute-start(f32[16,4096]{1,0:T(8,128)S(1)} %add.120), channel_id=1, source_target_pairs={{0,2},{1,3},{2,0},{3,1},{4,6},{5,7},{6,4},{7,5}} | collective-permute-start | bytes 786440 | tf_op jit(solution)/shard_map/ppermute | solution.py:426
  456.4 2.3 copy-start.1

commit v3 on v2

--- a/solution.py
+++ b/solution.py
@@ -8,6 +8,8 @@
 from jax.sharding import PartitionSpec as P
 
 
+FOUR = range(4)
+ORIGIN = (0, 0, 0)
 COLD = 64
 OVER = 128
 VMEM_LIMIT = 62 * 1024 * 1024
@@ -44,13 +46,15 @@
     x_out, do_out = take(1 * has_x), take(1 * has_g)
     if mode == "fwd":
         z_hbm = take(2)
-    hid, more = take(3 * has_g), take(3 * (mode == "grad"))
+    hid_hbm = take(3 * has_g) + take(3 * (mode == "grad"))
     acc = take(3 if mode == "both" else 2)
     zs = take(2 * (mode == "grad"))
     g_sc = take(1 * (mode == "grad"))
     sel, wbuf, wsem = take(3)
     zsem = take(1 * (mode != "both"))
     col = take(1 * has_g)
+    hid, more = take(3 * has_g), take(3 * (mode == "grad"))
+    hsem = take(1 * has_g)
     c = pl.program_id(0)
 
     def w_copies(f, expert, slot):
@@ -65,6 +69,10 @@
         if mode == "fwd":
             return [pltpu.make_async_copy(acc[n].at[i], z_hbm[n].at[i], zsem[0].at[n, i]) for n in range(2)]
         return [pltpu.make_async_copy(z_hbm[n].at[i], zs[n].at[i], zsem[0].at[n, i]) for n in range(2)]
+
+    def hid_copies(tile):
+        return [pltpu.make_async_copy(v.at[tile], o.at[tile], hsem[0].at[n, tile])
+                for n, (v, o) in enumerate(zip(hid + more, hid_hbm))]
 
     def each_active(fn):
         for i in range(8):
@@ -82,7 +90,7 @@
 
     @pl.when(c == 0)
     def _():
-        for k in range(4):
+        for k in FOUR:
             for m in range(5):
                 n = OVER if m == 4 else COLD
                 lo = COLD * m
@@ -93,11 +101,11 @@
                     col[0][k, lo:lo + n, :] = jnp.sum(jnp.where(hit, gates[k, m:m + 1, :], 0.0), axis=1, keepdims=True)
 
     def put(out, k, rows):
-        for j in range(4):
+        for j in FOUR:
             out[j, COLD * k:COLD * (k + 1), :] = rows[COLD * j:COLD * (j + 1)]
         out[4 + k // 2, OVER * (k % 2):OVER * (k % 2) + OVER, :] = rows[256:384]
 
-    for k in range(4):
+    for k in FOUR:
         if has_x:
             put(x_out[0], k, mm(sel[k], xs[k][...], NN).astype(BF16))
         if has_g:
@@ -180,6 +188,12 @@
                     finish(i, tile, 0)
 
                 finish(i, tile, 128)
+                second = act[jnp.minimum(i + 1, 7)]
+
+                @pl.when((i < 4) | (i == 5) | (i == 7) | (second == 0))
+                def _():
+                    for copy in hid_copies(tile):
+                        copy.start()
 
         return 0
 
@@ -189,6 +203,12 @@
         @pl.when(c == n_c - 1)
         def _():
             each_active(lambda i: [copy.wait() for copy in z_copies(i)])
+    else:
+        @pl.when(c == n_c - 1)
+        def _():
+            for tile in range(6):
+                for copy in hid_copies(tile):
+                    copy.wait()
 
 
 def experts(mode, eidx, act, slots, gates, xs, gs, weights, zs, dc, ring):
@@ -196,21 +216,17 @@
     ff, dim = weights[0].shape[1:]
     n_c = dim // dc
     any_blk = pl.BlockSpec(memory_space=pl.ANY)
-    small = pl.BlockSpec((4, 8, 256), lambda c, e, t: (0, 0, 0))
+    small = pl.BlockSpec((4, 8, 256), lambda c, e, t: ORIGIN)
     v_blk = pl.BlockSpec((256, dc), lambda c, e, t: (0, c))
-
-    def whole(d0, d1, dtype):
-        return (jax.ShapeDtypeStruct((6, d0, d1), dtype),
-                pl.BlockSpec((6, d0, d1), lambda c, e, t: (0, 0, 0), pipeline_mode=pl.Buffered(1)))
 
     outs = [(jax.ShapeDtypeStruct((6, 256, dim), BF16),
              pl.BlockSpec((6, 256, dc), lambda c, e, t: (0, 0, c)))] * (has_x + has_g)
     if mode == "fwd":
         outs += [(jax.ShapeDtypeStruct((8, ff, 256), F32), any_blk)] * 2
-    if has_g:
-        outs += [whole(ff, 256, BF16)] * 3
+    hid = [((6, ff, 256), BF16)] * (3 * has_g)
     if mode == "grad":
-        outs += [whole(8, 256, F32), whole(256, ff, BF16), whole(256, ff, BF16)]
+        hid += [((6, 8, 256), F32)] + [((6, 256, ff), BF16)] * 2
+    outs += [(jax.ShapeDtypeStruct(*h), any_blk) for h in hid]
     n_acc = 3 if mode == "both" else 2
     scratch = [pltpu.VMEM((8, ff, 256), F32)] * (n_acc + len(zs))
     if mode == "grad":
@@ -220,6 +236,7 @@
         scratch.append(pltpu.SemaphoreType.DMA((2, 8)))
     if has_g:
         scratch.append(pltpu.VMEM((4, 384, 1), F32))
+        scratch += [pltpu.VMEM(*h) for h in hid] + [pltpu.SemaphoreType.DMA((len(hid), 6))]
     n_v = len(xs) + len(gs)
     n_mm = 4 if mode == "both" else 2
     return pl.pallas_call(
@@ -234,9 +251,9 @@
     )(eidx, act, slots, gates, *xs, *gs, *weights, *zs)
 
 
-def back_kernel(n_c, dc, ring, eidx, act, d1, d3, w1_hbm, w3_hbm, s0, s1, s2, s3, o0, o1, o2, o3, r_sc, sel, wbuf, wsem):
+def back_kernel(n_c, dc, ring, eidx, act, d1, d3, w1_hbm, w3_hbm, slots, o0, o1, o2, o3, r_sc, sel, wbuf, wsem):
     c = pl.program_id(0)
-    slots, outs = (s0, s1, s2, s3), (o0, o1, o2, o3)
+    outs = (o0, o1, o2, o3)
 
     def w_copies(f, expert, slot):
         cols = pl.ds(pl.multiple_of((f // 4) * dc, dc), dc)
@@ -252,10 +269,10 @@
             for copy in ring_copies(jnp.int32(f)):
                 copy.start()
         lane = lax.broadcasted_iota(jnp.int32, (256, 384), 1).astype(F32)
-        for k in range(4):
-            hit = lane == slots[k][:, 0:1]
+        for k in FOUR:
+            hit = lane == slots[k, :, :1]
             for m in range(1, 5):
-                hit = hit | (lane == slots[k][:, m:m + 1])
+                hit = hit | (lane == slots[k, :, m:m + 1])
             sel[k] = jnp.where(hit, 1.0, 0.0).astype(BF16)
 
     def step(i, _):
@@ -289,7 +306,7 @@
             @pl.when(i < 4)
             def _():
                 lo = pl.multiple_of(expert * COLD, COLD)
-                for k in range(4):
+                for k in FOUR:
                     r_sc[k, pl.ds(lo, COLD), :] = r[COLD * k:COLD * (k + 1)]
 
             for q in range(2):
@@ -304,7 +321,7 @@
         return 0
 
     lax.fori_loop(0, 8, step, 0)
-    for k in range(4):
+    for k in FOUR:
         outs[k][...] = mm(sel[k], r_sc[k], NN)
 
 
@@ -312,14 +329,14 @@
     ff, dim = w1t.shape[1:]
     dc, ring = 1024, 4
     n_c = dim // dc
-    d_blk = pl.BlockSpec((6, 256, ff), lambda c, e, t: (0, 0, 0), pipeline_mode=pl.Buffered(1))
+    d_blk = pl.BlockSpec((6, 256, ff), lambda c, e, t: ORIGIN, pipeline_mode=pl.Buffered(1))
     any_blk = pl.BlockSpec(memory_space=pl.ANY)
-    s_blk = pl.BlockSpec((256, 8), lambda c, e, t: (0, 0))
+    s_blk = pl.BlockSpec((4, 256, 8), lambda c, e, t: ORIGIN)
     return pl.pallas_call(
         functools.partial(back_kernel, n_c, dc, ring),
         grid_spec=pltpu.PrefetchScalarGridSpec(
             num_scalar_prefetch=2, grid=(n_c,),
-            in_specs=[d_blk, d_blk, any_blk, any_blk] + [s_blk] * 4,
+            in_specs=[d_blk, d_blk, any_blk, any_blk, s_blk],
             out_specs=[pl.BlockSpec((256, dc), lambda c, e, t: (0, c))] * 4,
             scratch_shapes=[pltpu.VMEM((4, 384, dc), BF16), pltpu.VMEM((4, 256, 384), BF16),
                             pltpu.VMEM((ring + 1, 2, ff, dc), BF16), pltpu.SemaphoreType.DMA((ring + 1, 2))]),
@@ -327,7 +344,7 @@
         compiler_params=pltpu.CompilerParams(vmem_limit_bytes=VMEM_LIMIT),
         cost_estimate=cost(2 * 2 * 1536 * dim * ff, 70e6),
         name="back",
-    )(eidx, act, d1, d3, w1t, w3t, *slots)
+    )(eidx, act, d1, d3, w1t, w3t, slots)
 
 
 def wgrad_kernel(info, xa, xb, ga, gb, xoa, xob, goa, gob,
@@ -402,7 +419,7 @@
 
     main_blk = pl.BlockSpec((1, 256, dc), lambda c, j, s: (j, 0, c))
     over_blk = pl.BlockSpec((2, 256, dc), lambda c, j, s: (2, 0, c))
-    hid_blk = pl.BlockSpec((6, ff, 256), lambda c, j, s: (0, 0, 0), pipeline_mode=pl.Buffered(1))
+    hid_blk = pl.BlockSpec((6, ff, 256), lambda c, j, s: ORIGIN, pipeline_mode=pl.Buffered(1))
     return pl.pallas_call(
         wgrad_kernel,
         grid_spec=pltpu.PrefetchScalarGridSpec(
@@ -467,7 +484,7 @@
         g_across = shift(dy_loc, 0, 2)
         g_sib = shift(dy_loc, 0, 1)
         g_y = shift(dy_loc, 1, 0)
-        idx_b = jnp.stack([shift(idx_t, 1, k) for k in range(4)])
+        idx_b = jnp.stack([shift(idx_t, 1, k) for k in FOUR])
 
         logits = jnp.dot(x_loc, w_router, preferred_element_type=F32)
         hit = route_idx[:, :, None] == jnp.arange(16, dtype=jnp.int32)
@@ -475,25 +492,27 @@
         probs = jax.nn.softmax(chosen, axis=-1)
         gate_t = jnp.sum(jnp.where(hit, probs[:, :, None], 0.0), axis=1).T
         gates_a = [gate_t] + [shift(gate_t, 0, k) for k in (1, 2, 3)]
-        gates_b = [shift(gate_t, 1, k) for k in range(4)]
+        gates_b = [shift(gate_t, 1, k) for k in FOUR]
 
         ranks_a, slots_a, hot_a, eidx_a, act_a = tables(idx_a)
+        slots_t = jnp.swapaxes(slots_a, 1, 2)
         x_across_sib = shift(x_across, 0, 1)
         x_ya = shift(x_across, 1, 0)
         x_ys = shift(x_y, 0, 1)
         gate_a0 = jnp.zeros((4, 8, tok), F32)
         xa, z1_a, z3_a = experts("fwd", eidx_a, act_a, slots_a, gate_a0, (x_loc, x_sib, x_across, x_across_sib), (),
                                  (w1t, w3t), (), 2048, 3)
-        z1_a, g_across, g_y, gates_a, gates_b, idx_b = lax.optimization_barrier((z1_a, g_across, g_y, gates_a, gates_b, idx_b))
+        z1_a, g_across, g_y = lax.optimization_barrier((z1_a, g_across, g_y))
+        z3_a, gates_a, gates_b, idx_b = lax.optimization_barrier((z3_a, gates_a, gates_b, idx_b))
         ranks_b, slots_b, hot_b, eidx_b, act_b = tables(idx_b)
         g_across_sib = shift(g_across, 0, 1)
         g_ya = shift(g_across, 1, 0)
         g_ys = shift(g_y, 0, 1)
         gate_a = gate_table(gates_a, ranks_a)
+        gate_b = gate_table(gates_b, ranks_b)
         da, a_a, d1_a, d3_a, q_a, d1r_a, d3r_a = experts(
             "grad", eidx_a, act_a, slots_a, gate_a, (), (dy_loc, g_sib, g_across, g_across_sib), (w2,), (z1_a, z3_a), 1024, 4)
-        slots_t = jnp.swapaxes(slots_a, 1, 2)
-        part = back(eidx_a, act_a, d1r_a, d3r_a, w1t, w3t, [slots_t[k] for k in range(4)])
+        part = back(eidx_a, act_a, d1r_a, d3r_a, w1t, w3t, slots_t)
 
         q_rows = q_a[:, 0, :]
         q_main = q_rows[:4].reshape(4, 4, COLD).transpose(1, 0, 2)
@@ -507,7 +526,6 @@
         part_own, x_ya, g_ya, q_recv = lax.optimization_barrier((part[0], x_ya, g_ya, q_recv))
         x_yas = shift(x_ya, 0, 1)
         g_yas = shift(g_ya, 0, 1)
-        gate_b = gate_table(gates_b, ranks_b)
 
         to_sib = shift(part[1], 0, 1)
         pair = part[2] + shift(part[3], 0, 1)
@@ -524,7 +542,7 @@
         gr_recv = shift(gr, 1, 0)
         xb, db, a_b, d1_b, d3_b = experts(
             "both", eidx_b, act_b, slots_b, gate_b, (x_y, x_ys, x_ya, x_yas), (g_y, g_ys, g_ya, g_yas),
-            (w1t, w3t, w2), (), 512, 4)
+            (w1t, w3t, w2), (), 512, 6)
         d1_b, gr_recv = lax.optimization_barrier((d1_b, gr_recv))
         gr = gr + gr_recv
         gr_recv = shift(gr, 0, 2)

time: 465 us -> 429 us (0.923)
  waiting for transfers between devices: 143 us -> 111 us
    ppermute x37, waiting for transfers between devices: 143 us -> 111 us  [shift(): return lax.ppermute(arr, axes, pairs)]
  transfers between devices with their start and end apart: 37 -> 37, of which waited for: 9 -> 14; matrix products, arithmetic and copies ran while one was open for 6% -> 7% of each run, Pallas kernels for 54% -> 58%
where the time goes in v3:
time: 429 us; the launch traced here: 428 us
  Pallas kernels  249 us (58%)
  waiting for transfers between devices  111 us (26%)
  starting transfers between devices  26.3 us (6%)
  other arithmetic  22.9 us (5%)
  local copies, waits for them, and re-layouts  7.37 us (2%)
  between operations  6.07 us (1%)
  matrix products  5.27 us (1%)
    pallas_call x3, Pallas kernels, experts(): pl.pallas_call(functools.partial(expert_kernel, mode, n_c, dc, ring), gri...  130 us
    ppermute x37, waiting for transfers between devices, shift(): return lax.ppermute(arr, axes, pairs)  111 us
    pallas_call x1, Pallas kernels, wgrad(): pl.pallas_call(wgrad_kernel, grid_spec=pltpu.PrefetchScalarGridSpec(num_s...  81.1 us
    pallas_call x1, Pallas kernels, back(): pl.pallas_call(functools.partial(back_kernel, n_c, dc, ring), grid_spec=p...  37.8 us
    ppermute x37, starting transfers between devices, shift(): return lax.ppermute(arr, axes, pairs)  26.3 us
  transfers between devices with their start and end apart: 37, of which 14 were waited for; matrix products, arithmetic and copies ran while one was open for 7% of the time, Pallas kernels for 58%

profile of v3, /device:TPU:0, one launch (start us, length us, event | category | flops | bytes accessed | tf_op | source)
XLA Modules:
  0.0 428.0 jit_solution(16648302895207504218)
XLA Ops:
  0.6 3.3 collective-permute-start.4
  4.0 45.9 %collective-permute-done.4.refs_2_ = bf16[256,4096]{1,0:T(8,128)(2,1)} collective-permute-done((bf16[256,4096]{1,0:T(8,128)(2,1)}, bf16[256,4096]{1,0:T(8,128)(2,1)}, u32[]{:S(2)}, u32[]{:S(2)}) %collective-permute-start.4) | collective-permute-done | bytes 2097184 | tf_op jit(solution)/shard_map/ppermute | solution.py:443
  49.9 1.8 collective-permute-start.2
  52.2 1.2 collective-permute-done.2
  53.3 1.6 collective-permute-start.18
  54.9 0.7 collective-permute-done.1
  55.6 1.5 collective-permute-start.19
  57.1 0.7 pad_add_fusion
  61.5 0.7 stack.99.act
  62.9 1.3 pad_add_fusion.2.eidx
  65.4 33.0 %shard_map.110 = (bf16[6,256,4096]{2,1,0:T(8,128)(2,1)}, f32[8,688,256]{2,1,0:T(8,128)}, f32[8,688,256]{2,1,0:T(8,128)}) custom-call(s32[8]{0:T(128)} %pad_add_fusion.2.eidx, s32[8]{0:T(128)} %stack.99.act, f32[4,8,256]{2,1,0:T(8,128)} %get-tuple-element.113.slots, f32[4,8,256]{2,1,0:T(8,128)} %broadcast_in_dim.122.gates, bf16[256,4096]{1,0:T(8,128)(2,1)} %refs_0_.2, ...), custom_call_target="tpu_custom_call" | custom-call | flops 17314086912 | bytes 90000000 | tf_op jit(solution)/shard_map/pallas_call | solution.py:242
  98.4 3.1 collective-permute-done.18.refs_2_
  101.5 2.4 collective-permute-done.19.refs_4_
  104.0 2.2 fusion.16
  106.3 1.6 collective-permute-start.12
  108.0 1.4 collective-permute-start.15
  109.4 0.8 collective-permute-start.14
  110.2 2.2 collective-permute-done.15
  112.7 0.9 collective-permute-start.16
  113.6 2.5 collective-permute-done.13
  116.1 1.4 collective-permute-start.11
  117.5 1.6 collective-permute-start.9
  119.2 1.7 collective-permute-done.11
  120.9 1.4 collective-permute-start.7
  122.7 1.0 copy.16.slots
  124.7 1.4 collective-permute-start.22
  126.7 0.7 maximum_maximum_fusion.1
  127.4 40.1 %shard_map.111 = (bf16[6,256,4096]{2,1,0:T(8,128)(2,1)}, bf16[6,688,256]{2,1,0:T(8,128)(2,1)}, bf16[6,688,256]{2,1,0:T(8,128)(2,1)}, bf16[6,688,256]{2,1,0:T(8,1...) custom-call(s32[8]{0:T(128)} %pad_add_fusion.2.eidx, s32[8]{0:T(128)} %stack.99.act, ...), custom_call_target="tpu_custom_call" | custom-call | flops 17314086912 | bytes 90000000 | tf_op jit(solution)/shard_map/pallas_call | solution.py:242
  167.5 37.8 %back.1 = (f32[256,4096]{1,0:T(8,128)}, f32[256,4096]{1,0:T(8,128)}, f32[256,4096]{1,0:T(8,128)}, f32[256,4096]{1,0:T(8,128)}) custom-call(s32[8]{0:T(128)} %pad_add_fusion.2.eidx, s32[8]{0:T(128)} %stack.99.act, bf16[6,256,688]{2,1,0:T(8,128)(2,1)} %get-tuple-element.65.d1, bf16[6,256,688]{2,1,0:T(8,128)(2,1)} %get-tuple-element.66.d3, ...), custom_call_target="tpu_custom_call" | custom-call | flops 17314086912 | bytes 70000000 | tf_op jit(solution)/shard_map/back/pallas_call | solution.py:335
  206.0 0.7 slice.56
  206.7 0.8 slice_reduce_fusion
  207.8 1.5 select_reduce_fusion
  209.3 1.2 collective-permute-start.25
  211.1 6.7 %collective-permute-done.22.refs_6_ = bf16[256,4096]{1,0:T(8,128)(2,1)} collective-permute-done((bf16[256,4096]{1,0:T(8,128)(2,1)}, bf16[256,4096]{1,0:T(8,128)(2,1)}, u32[]{:S(2)}, u32[]{:S(2)}) %collective-permute-start.22) | collective-permute-done | bytes 2097184 | tf_op jit(solution)/shard_map/ppermute | solution.py:443
  217.9 1.2 collective-permute-done.23
  219.5 42.4 %collective-permute-done.27.refs_0_ = bf16[256,4096]{1,0:T(8,128)(2,1)} collective-permute-done((bf16[256,4096]{1,0:T(8,128)(2,1)}, bf16[256,4096]{1,0:T(8,128)(2,1)}, u32[]{:S(2)}, u32[]{:S(2)}) %collective-permute-start.27) | collective-permute-done | bytes 2097184 | tf_op jit(solution)/shard_map/ppermute | solution.py:443
  265.0 2.0 fusion.17
  267.0 6.0 %add.117 = f32[256,4096]{1,0:T(8,128)} add(f32[256,4096]{1,0:T(8,128)} %get-tuple-element.79, f32[256,4096]{1,0:T(8,128)} %collective-permute-done.31) | non-fusion elementwise | flops 1048576 | bytes 12582912 | tf_op jit(solution)/shard_map/add | solution.py:531
  273.1 1.1 pad_add_fusion.4.eidx
  277.3 0.7 maximum_maximum_fusion.2.slots
  278.5 1.0 collective-permute-start.36
  280.1 57.0 %shard_map.112 = (bf16[6,256,4096]{2,1,0:T(8,128)(2,1)}, bf16[6,256,4096]{2,1,0:T(8,128)(2,1)}, bf16[6,688,256]{2,1,0:T(8,128)(2,1)}, bf16[6,688,256]{2,1,0:T(8,128)(2,1)}, bf16[6,688,256]{2,1,0:T(8,128)(2,1)}) custom-call(s32[8]{0:T(128)} %pad_add_fusion.4.eidx, s32[8]{0:T(128)} %stack.112.act, f32[4,8,256]{2,1,0:T(8,128)} %maximum_maximum_fusion.2.slots, ...), custom_call_target="tpu_custom_call" | custom-call | flops 34628173824 | bytes 90000000 | tf_op jit(solution)/shard_map/pallas_call | solution.py:242
  337.2 0.9 collective-permute-start.35
  338.1 81.1 %wgrad.1 = (f32[4,688,4096]{2,1,0:T(8,128)}, f32[4,688,4096]{2,1,0:T(8,128)}, f32[4,688,4096]{2,1,0:T(8,128)}) custom-call(s32[9]{0:T(128)} %pad_add_fusion.3.info, bf16[6,256,4096]{2,1,0:T(8,128)(2,1)} %get-tuple-element.72.xa.xoa, bf16[6,256,4096]{2,1,0:T(8,128)(2,1)} %get-tuple-element.87.xb.xob, bf16[6,256,4096]{2,1,0:T(8,128)(2,1)} %get-tuple-element.88.ga.goa, ...), custom_call_target="tpu_custom_call" | custom-call | flops 51942260736 | bytes 200000000 | tf_op jit(solution)/shard_map/wgrad/pallas_call | solution.py:423
  419.2 0.7 fusion.18
  420.0 0.7 add_bitcast_fusion
  420.7 0.8 copy-done.1
  421.5 6.5 %add_convert_fusion = bf16[256,4096]{1,0:T(8,128)(2,1)} fusion(f32[256,4096]{1,0:T(8,128)S(1)} %fusion.18, f32[256,4096]{1,0:T(8,128)} %collective-permute-done.36, f32[256,4096]{1,0:T(8,128)S(1)} %copy-done.1, f32[256,4096]{1,0:T(8,128)} %collective-permute-done.26), kind=kLoop, calls=%fused_computation.1 | loop fusion | flops 4194304 | bytes 18874368 | tf_op jit(solution)/shard_map/convert_element_type | solution.py:554
  (106 shorter events, 12.9 us)
Async XLA Ops:
  0.6 103.3 %copy-start = (bf16[4096,16]{0,1:T(8,128)(2,1)S(1)}, bf16[4096,16]{0,1:T(8,128)(2,1)}, u32[]{:S(2)}) copy-start(bf16[4096,16]{0,1:T(8,128)(2,1)} %param.9) | copy-start | bytes 393220
  0.6 49.3 %collective-permute-start.4 = (bf16[256,4096]{1,0:T(8,128)(2,1)}, bf16[256,4096]{1,0:T(8,128)(2,1)}, u32[]{:S(2)}, u32[]{:S(2)}) collective-permute-start(bf16[256,4096]{1,0:T(8,128)(2,1)} %refs_0_.2), channel_id=1, source_target_pairs={{0,2},{1,3},{2,0},{3,1},{4,6},{5,7},{6,4},{7,5}} | collective-permute-start | bytes 6291464 | tf_op jit(solution)/shard_map/ppermute | solution.py:443
  4.0 60.8 %collective-permute-start.3 = (bf16[256,4096]{1,0:T(8,128)(2,1)}, bf16[256,4096]{1,0:T(8,128)(2,1)}, u32[]{:S(2)}, u32[]{:S(2)}) collective-permute-start(bf16[256,4096]{1,0:T(8,128)(2,1)} %refs_0_.2), channel_id=1, source_target_pairs={{0,1},{1,0},{2,3},{3,2},{4,5},{5,4},{6,7},{7,6}} | collective-permute-start | bytes 6291464 | tf_op jit(solution)/shard_map/ppermute | solution.py:443
  49.9 14.9 %collective-permute-start.5 = (bf16[256,4096]{1,0:T(8,128)(2,1)}, bf16[256,4096]{1,0:T(8,128)(2,1)}, u32[]{:S(2)}, u32[]{:S(2)}) collective-permute-start(bf16[256,4096]{1,0:T(8,128)(2,1)} %collective-permute-done.4.refs_2_), channel_id=1, source_target_pairs={{0,1},{1,0},{2,3},{3,2},{4,5},{5,4},{6,7},{7,6}} | collective-permute-start | bytes 6291464 | tf_op jit(solution)/shard_map/ppermute | solution.py:443
  49.9 3.4 collective-permute-start.2
  51.8 3.8 collective-permute-start.1
  52.1 3.5 collective-permute-start
  53.3 48.2 %collective-permute-start.18 = (bf16[256,4096]{1,0:T(8,128)(2,1)}, bf16[256,4096]{1,0:T(8,128)(2,1)}, u32[]{:S(2)}, u32[]{:S(2)}) collective-permute-start(bf16[256,4096]{1,0:T(8,128)(2,1)} %refs_0_.3), channel_id=1, source_target_pairs={{0,2},{1,3},{2,0},{3,1},{4,6},{5,7},{6,4},{7,5}} | collective-permute-start | bytes 6291464 | tf_op jit(solution)/shard_map/ppermute | solution.py:443
  55.6 71.8 %collective-permute-start.17 = (bf16[256,4096]{1,0:T(8,128)(2,1)}, bf16[256,4096]{1,0:T(8,128)(2,1)}, u32[]{:S(2)}, u32[]{:S(2)}) collective-permute-start(bf16[256,4096]{1,0:T(8,128)(2,1)} %refs_0_.3), channel_id=1, source_target_pairs={{0,1},{1,0},{2,3},{3,2},{4,5},{5,4},{6,7},{7,6}} | collective-permute-start | bytes 6291464 | tf_op jit(solution)/shard_map/ppermute | solution.py:443
  55.6 48.4 %collective-permute-start.19 = (bf16[256,4096]{1,0:T(8,128)(2,1)}, bf16[256,4096]{1,0:T(8,128)(2,1)}, u32[]{:S(2)}, u32[]{:S(2)}) collective-permute-start(bf16[256,4096]{1,0:T(8,128)(2,1)} %refs_0_.3), channel_id=1, source_target_pairs={{0,4},{1,5},{2,6},{3,7},{4,0},{5,1},{6,2},{7,3}} | collective-permute-start | bytes 6291464 | tf_op jit(solution)/shard_map/ppermute | solution.py:443
  98.4 7.8 %copy-start.2 = (s32[256,4]{0,1:T(4,128)S(1)}, s32[256,4]{0,1:T(4,128)}, u32[]{:S(2)}) copy-start(s32[256,4]{0,1:T(4,128)} %param.8) | copy-start | bytes 12292
  104.0 23.4 %collective-permute-start.20 = (bf16[256,4096]{1,0:T(8,128)(2,1)}, bf16[256,4096]{1,0:T(8,128)(2,1)}, u32[]{:S(2)}, u32[]{:S(2)}) collective-permute-start(bf16[256,4096]{1,0:T(8,128)(2,1)} %collective-permute-done.18.refs_2_), channel_id=1, source_target_pairs={{0,1},{1,0},{2,3},{3,2},{4,5},{5,4},{6,7},{7,6}} | collective-permute-start | bytes 6291464 | tf_op jit(solution)/shard_map/ppermute | solution.py:443
  106.3 11.2 %collective-permute-start.12 = (f32[16,256]{1,0:T(8,128)S(1)}, f32[16,256]{1,0:T(8,128)S(1)}, u32[]{:S(2)}, u32[]{:S(2)}) collective-permute-start(f32[16,256]{1,0:T(8,128)S(1)} %bitcast.73), channel_id=1, source_target_pairs={{0,7},{1,6},{2,5},{3,4},{4,3},{5,2},{6,1},{7,0}} | collective-permute-start | bytes 49160 | tf_op jit(solution)/shard_map/ppermute | solution.py:443
  108.0 4.5 %collective-permute-start.15 = (s32[4,256]{1,0:T(4,128)S(1)}, s32[4,256]{1,0:T(4,128)S(1)}, u32[]{:S(2)}, u32[]{:S(2)}) collective-permute-start(s32[4,256]{1,0:T(4,128)S(1)} %bitcast.85), channel_id=1, source_target_pairs={{0,6},{1,7},{2,4},{3,5},{4,2},{5,3},{6,0},{7,1}} | collective-permute-start | bytes 12296 | tf_op jit(solution)/shard_map/ppermute | solution.py:443
  109.4 3.4 collective-permute-start.14
  112.5 3.6 collective-permute-start.13
  112.7 4.8 %collective-permute-start.16 = (s32[4,256]{1,0:T(4,128)S(1)}, s32[4,256]{1,0:T(4,128)S(1)}, u32[]{:S(2)}, u32[]{:S(2)}) collective-permute-start(s32[4,256]{1,0:T(4,128)S(1)} %bitcast.88), channel_id=1, source_target_pairs={{0,7},{1,6},{2,5},{3,4},{4,3},{5,2},{6,1},{7,0}} | collective-permute-start | bytes 12296 | tf_op jit(solution)/shard_map/ppermute | solution.py:443
  116.1 4.7 %collective-permute-start.11 = (f32[16,256]{1,0:T(8,128)S(1)}, f32[16,256]{1,0:T(8,128)S(1)}, u32[]{:S(2)}, u32[]{:S(2)}) collective-permute-start(f32[16,256]{1,0:T(8,128)S(1)} %bitcast.74), channel_id=1, source_target_pairs={{0,6},{1,7},{2,4},{3,5},{4,2},{5,3},{6,0},{7,1}} | collective-permute-start | bytes 49160 | tf_op jit(solution)/shard_map/ppermute | solution.py:443
  117.5 3.4 collective-permute-start.10
  117.5 4.8 %collective-permute-start.9 = (f32[16,256]{1,0:T(8,128)S(1)}, f32[16,256]{1,0:T(8,128)S(1)}, u32[]{:S(2)}, u32[]{:S(2)}) collective-permute-start(f32[16,256]{1,0:T(8,128)S(1)} %bitcast.76), channel_id=1, source_target_pairs={{0,4},{1,5},{2,6},{3,7},{4,0},{5,1},{6,2},{7,3}} | collective-permute-start | bytes 49160 | tf_op jit(solution)/shard_map/ppermute | solution.py:443
  120.8 3.3 collective-permute-start.8
  120.9 3.7 collective-permute-start.7
  122.3 3.8 collective-permute-start.6
  124.1 86.4 %collective-permute-start.21 = (bf16[256,4096]{1,0:T(8,128)(2,1)}, bf16[256,4096]{1,0:T(8,128)(2,1)}, u32[]{:S(2)}, u32[]{:S(2)}) collective-permute-start(bf16[256,4096]{1,0:T(8,128)(2,1)} %collective-permute-done.4.refs_2_), channel_id=1, source_target_pairs={{0,4},{1,5},{2,6},{3,7},{4,0},{5,1},{6,2},{7,3}} | collective-permute-start | bytes 6291464 | tf_op jit(solution)/shard_map/ppermute | solution.py:443
  124.7 93.2 %collective-permute-start.22 = (bf16[256,4096]{1,0:T(8,128)(2,1)}, bf16[256,4096]{1,0:T(8,128)(2,1)}, u32[]{:S(2)}, u32[]{:S(2)}) collective-permute-start(bf16[256,4096]{1,0:T(8,128)(2,1)} %collective-permute-done.18.refs_2_), channel_id=1, source_target_pairs={{0,4},{1,5},{2,6},{3,7},{4,0},{5,1},{6,2},{7,3}} | collective-permute-start | bytes 6291464 | tf_op jit(solution)/shard_map/ppermute | solution.py:443
  205.3 61.7 %collective-permute-start.31 = (f32[256,4096]{1,0:T(8,128)}, f32[256,4096]{1,0:T(8,128)}, u32[]{:S(2)}, u32[]{:S(2)}) collective-permute-start(f32[256,4096]{1,0:T(8,128)} %get-tuple-element.80), channel_id=1, source_target_pairs={{0,1},{1,0},{2,3},{3,2},{4,5},{5,4},{6,7},{7,6}} | collective-permute-start | bytes 12582920 | tf_op jit(solution)/shard_map/ppermute | solution.py:443
  205.3 56.6 %collective-permute-start.27 = (bf16[256,4096]{1,0:T(8,128)(2,1)}, bf16[256,4096]{1,0:T(8,128)(2,1)}, u32[]{:S(2)}, u32[]{:S(2)}) collective-permute-start(bf16[256,4096]{1,0:T(8,128)(2,1)} %refs_0_.2), channel_id=1, source_target_pairs={{0,4},{1,5},{2,6},{3,7},{4,0},{5,1},{6,2},{7,3}} | collective-permute-start | bytes 6291464 | tf_op jit(solution)/shard_map/ppermute | solution.py:443
  209.3 8.5 %collective-permute-start.25 = (f32[4,256]{1,0:T(4,128)S(1)}, f32[4,256]{1,0:T(4,128)S(1)}, u32[]{:S(2)}, u32[]{:S(2)}) collective-permute-start(f32[4,256]{1,0:T(4,128)S(1)} %get-tuple-element.115), channel_id=1, source_target_pairs={{0,3},{1,2},{2,1},{3,0},{4,7},{5,6},{6,5},{7,4}} | collective-permute-start | bytes 12296 | tf_op jit(solution)/shard_map/ppermute | solution.py:443
  210.5 7.4 %collective-permute-start.24 = (f32[4,256]{1,0:T(4,128)S(1)}, f32[4,256]{1,0:T(4,128)S(1)}, u32[]{:S(2)}, u32[]{:S(2)}) collective-permute-start(f32[4,256]{1,0:T(4,128)S(1)} %get-tuple-element.116), channel_id=1, source_target_pairs={{0,2},{1,3},{2,0},{3,1},{4,6},{5,7},{6,4},{7,5}} | collective-permute-start | bytes 12296 | tf_op jit(solution)/shard_map/ppermute | solution.py:443
  217.9 1.2 collective-permute-start.23
  219.0 54.0 %collective-permute-start.29 = (bf16[256,4096]{1,0:T(8,128)(2,1)}, bf16[256,4096]{1,0:T(8,128)(2,1)}, u32[]{:S(2)}, u32[]{:S(2)}) collective-permute-start(bf16[256,4096]{1,0:T(8,128)(2,1)} %collective-permute-done.21.refs_2_), channel_id=1, source_target_pairs={{0,1},{1,0},{2,3},{3,2},{4,5},{5,4},{6,7},{7,6}} | collective-permute-start | bytes 6291464 | tf_op jit(solution)/shard_map/ppermute | solution.py:443
  219.2 53.9 %collective-permute-start.30 = (bf16[256,4096]{1,0:T(8,128)(2,1)}, bf16[256,4096]{1,0:T(8,128)(2,1)}, u32[]{:S(2)}, u32[]{:S(2)}) collective-permute-start(bf16[256,4096]{1,0:T(8,128)(2,1)} %collective-permute-done.22.refs_6_), channel_id=1, source_target_pairs={{0,1},{1,0},{2,3},{3,2},{4,5},{5,4},{6,7},{7,6}} | collective-permute-start | bytes 6291464 | tf_op jit(solution)/shard_map/ppermute | solution.py:443
  261.9 18.2 %collective-permute-start.28 = (bf16[256,4096]{1,0:T(8,128)(2,1)}, bf16[256,4096]{1,0:T(8,128)(2,1)}, u32[]{:S(2)}, u32[]{:S(2)}) collective-permute-start(bf16[256,4096]{1,0:T(8,128)(2,1)} %collective-permute-done.27.refs_0_), channel_id=1, source_target_pairs={{0,1},{1,0},{2,3},{3,2},{4,5},{5,4},{6,7},{7,6}} | collective-permute-start | bytes 6291464 | tf_op jit(solution)/shard_map/ppermute | solution.py:443
  261.9 18.2 %collective-permute-start.32 = (bf16[256,4096]{1,0:T(8,128)(2,1)}, bf16[256,4096]{1,0:T(8,128)(2,1)}, u32[]{:S(2)}, u32[]{:S(2)}) collective-permute-start(bf16[256,4096]{1,0:T(8,128)(2,1)} %collective-permute-done.19.refs_4_), channel_id=1, source_target_pairs={{0,1},{1,0},{2,3},{3,2},{4,5},{5,4},{6,7},{7,6}} | collective-permute-start | bytes 6291464 | tf_op jit(solution)/shard_map/ppermute | solution.py:443
  273.1 6.4 %collective-permute-start.33 = (f32[16,4096]{1,0:T(8,128)S(1)}, f32[16,4096]{1,0:T(8,128)S(1)}, u32[]{:S(2)}, u32[]{:S(2)}) collective-permute-start(f32[16,4096]{1,0:T(8,128)S(1)} %fusion.17), channel_id=1, source_target_pairs={{0,1},{1,0},{2,3},{3,2},{4,5},{5,4},{6,7},{7,6}} | collective-permute-start | bytes 786440 | tf_op jit(solution)/shard_map/ppermute | solution.py:443
  278.0 142.7 %collective-permute-start.26 = (f32[256,4096]{1,0:T(8,128)}, f32[256,4096]{1,0:T(8,128)}, u32[]{:S(2)}, u32[]{:S(2)}) collective-permute-start(f32[256,4096]{1,0:T(8,128)} %get-tuple-element.70), channel_id=1, source_target_pairs={{0,1},{1,0},{2,3},{3,2},{4,5},{5,4},{6,7},{7,6}} | collective-permute-start | bytes 12582920 | tf_op jit(solution)/shard_map/ppermute | solution.py:443
  278.5 140.7 %collective-permute-start.36 = (f32[256,4096]{1,0:T(8,128)}, f32[256,4096]{1,0:T(8,128)}, u32[]{:S(2)}, u32[]{:S(2)}) collective-permute-start(f32[256,4096]{1,0:T(8,128)} %add.117), channel_id=1, source_target_pairs={{0,2},{1,3},{2,0},{3,1},{4,6},{5,7},{6,4},{7,5}} | collective-permute-start | bytes 12582920 | tf_op jit(solution)/shard_map/ppermute | solution.py:443
  279.5 57.6 %collective-permute-start.34 = (f32[16,4096]{1,0:T(8,128)S(1)}, f32[16,4096]{1,0:T(8,128)S(1)}, u32[]{:S(2)}, u32[]{:S(2)}) collective-permute-start(f32[16,4096]{1,0:T(8,128)S(1)} %add.119), channel_id=1, source_target_pairs={{0,4},{1,5},{2,6},{3,7},{4,0},{5,1},{6,2},{7,3}} | collective-permute-start | bytes 786440 | tf_op jit(solution)/shard_map/ppermute | solution.py:443
  337.2 82.0 %collective-permute-start.35 = (f32[16,4096]{1,0:T(8,128)S(1)}, f32[16,4096]{1,0:T(8,128)S(1)}, u32[]{:S(2)}, u32[]{:S(2)}) collective-permute-start(f32[16,4096]{1,0:T(8,128)S(1)} %add.120), channel_id=1, source_target_pairs={{0,2},{1,3},{2,0},{3,1},{4,6},{5,7},{6,4},{7,5}} | collective-permute-start | bytes 786440 | tf_op jit(solution)/shard_map/ppermute | solution.py:443
  419.2 2.3 copy-start.1
